TPU v7x, 32 devices: a whole 2x2x4 slice. The times are simulated.
32 devices in a mesh: dp: 2 (over x), b: 4 (over z), cp: 4 (over y, core).
Axes of the slice: x: 2, y: 2, z: 4, core: 2. Of those that a mesh axis runs over, the one named last changes fastest.
Arguments:
- x: bfloat16 [8, 2048, 2048], P(('dp', 'b'), 'cp'), parts along dimension 0
- ids: int32 [8, 2048, 12], P(('dp', 'b'), 'cp'), parts along dimension 0
- g_attn: bfloat16 [2048], replicated
- wq: bfloat16 [2048, 2048], replicated
- wk: bfloat16 [2048, 2048], replicated
- wv: bfloat16 [2048, 2048], replicated
- wo: bfloat16 [2048, 2048], replicated
- g_ffn: bfloat16 [2048], replicated
- w1: bfloat16 [2048, 8192], replicated
- w3: bfloat16 [2048, 8192], replicated
- w2: bfloat16 [8192, 2048], replicated
- g_moe: bfloat16 [2048], replicated
- wr: bfloat16 [2048, 96], replicated
- we_g: bfloat16 [64, 2048, 1024], P(('b', 'cp'))
- we_u: bfloat16 [64, 2048, 1024], P(('b', 'cp'))
- we_d: bfloat16 [64, 1024, 2048], P(('b', 'cp'))
Outputs:
- output: bfloat16 [8, 2048, 2048], P(('dp', 'b'), 'cp'), parts along dimension 0
There are 2 independent parts. A program takes and returns all parts, laid end to end along the dimension named above; an argument that names none is the same for every part.
All inputs are finite; a program needn't handle non-finite values.
Results may differ from a plain program's by a relative error of at most 0.00814887.
Values are sent between devices in bfloat16 or wider.
A program may use at most 1 GiB of HBM per device.

v0:
```python
import jax
import jax.numpy as jnp
from jax import lax
from jax.sharding import PartitionSpec as P

HEAD = 128
ROPE = 64
EPS = 1e-6
THETA = 10000.0
RSCALE = 2.5


def rms_norm(x, g):
    xf = x.astype(jnp.float32)
    r = lax.rsqrt(jnp.mean(xf * xf, axis=-1, keepdims=True) + EPS)
    return (xf * r * g.astype(jnp.float32)).astype(jnp.bfloat16)


def rope(t, pos):
    half = ROPE // 2
    freq = THETA ** (-jnp.arange(half, dtype=jnp.float32) / half)
    ang = pos.astype(jnp.float32)[:, None] * freq[None, :]
    c = jnp.cos(ang)[:, None, :]
    s = jnp.sin(ang)[:, None, :]
    tf = t.astype(jnp.float32)
    t1 = tf[..., :half]
    t2 = tf[..., half:ROPE]
    out = jnp.concatenate([t1 * c - t2 * s, t2 * c + t1 * s, tf[..., ROPE:]], axis=-1)
    return out.astype(jnp.bfloat16)


def proj(a, wt):
    return jnp.dot(a, wt, preferred_element_type=jnp.float32).astype(jnp.bfloat16)


def swiglu(z, wa, wb, wc):
    hh = (jax.nn.silu(jnp.dot(z, wa, preferred_element_type=jnp.float32)) * jnp.dot(z, wb, preferred_element_type=jnp.float32)).astype(jnp.bfloat16)
    return proj(hh, wc)


def attend(q, kb, vb, qpos, kpos, mx, den, acc):
    s = jnp.einsum('bkgqd,bskd->bkgqs', q, kb, preferred_element_type=jnp.float32) * (HEAD ** -0.5)
    s = jnp.where(qpos[:, None] >= kpos[None, :], s, -1e30)
    mnew = jnp.maximum(mx, jnp.max(s, axis=-1))
    corr = jnp.exp(mx - mnew)
    p = jnp.exp(s - mnew[..., None])
    den = den * corr + jnp.sum(p, axis=-1)
    pv = jnp.einsum('bkgqs,bskd->bkgqd', p.astype(jnp.bfloat16), vb, preferred_element_type=jnp.float32)
    acc = acc * corr[..., None] + pv
    return mnew, den, acc


def route(u, ids, wr, nexp):
    t = u.shape[0]
    top = ids.shape[-1]
    logits = jnp.dot(u, wr, preferred_element_type=jnp.float32)
    idf = ids.reshape(t, top)
    pick = idf[:, :, None] == jnp.arange(logits.shape[1])[None, None, :]
    gate = RSCALE * jax.nn.softmax(jnp.sum(jnp.where(pick, logits[:, None, :], 0.0), axis=-1), axis=-1)
    ffn = idf < nexp
    oh = pick[:, :, :nexp]
    cnt = jnp.sum(oh.astype(jnp.float32), axis=1)
    ti = jnp.arange(t)
    lower = (ti[None, :] < ti[:, None]).astype(jnp.bfloat16)
    excl = jnp.dot(lower, cnt.astype(jnp.bfloat16), preferred_element_type=jnp.float32)
    ji = jnp.arange(top)
    within = jnp.sum((idf[:, :, None] == idf[:, None, :]) & (ji[None, :] < ji[:, None])[None], axis=-1)
    rank = jnp.sum(jnp.where(oh, excl[:, None, :], 0.0), axis=-1).astype(jnp.int32) + within
    return gate, idf, ffn, rank, excl.T, (excl + cnt).T


def dispatch(u, first, last, cap):
    r = jnp.arange(cap, dtype=jnp.float32)[None, :, None]
    sel = ((r >= first[:, None, :]) & (r < last[:, None, :])).astype(jnp.bfloat16)
    return jnp.einsum('ect,td->ecd', sel, u, preferred_element_type=jnp.float32).astype(jnp.bfloat16)


def combine(got, gate, ffn, u):
    val = jnp.where(ffn[..., None], got.astype(jnp.float32), u.astype(jnp.float32)[:, None, :])
    return jnp.sum(gate[..., None] * val, axis=1)


def moe(u, ids, wr, we_g, we_u, we_d, ndev):
    t, d = u.shape
    top = ids.shape[-1]
    epd = we_g.shape[0]
    nexp = epd * ndev
    cap = t * top // nexp
    gate, idf, ffn, rank, first, last = route(u, ids, wr, nexp)
    idx = jnp.where(ffn, idf * cap + rank, 0)
    send = dispatch(u, first, last, cap).reshape(nexp * cap, d)
    recv = lax.all_to_all(send, ('b', 'cp'), 0, 0, tiled=True)
    xin = recv.reshape(ndev, epd, cap, d).transpose(1, 0, 2, 3).reshape(epd, ndev * cap, d)
    hg = jnp.einsum('ecd,edf->ecf', xin, we_g, preferred_element_type=jnp.float32)
    hu = jnp.einsum('ecd,edf->ecf', xin, we_u, preferred_element_type=jnp.float32)
    hh = (jax.nn.silu(hg) * hu).astype(jnp.bfloat16)
    yo = jnp.einsum('ecf,efd->ecd', hh, we_d, preferred_element_type=jnp.float32).astype(jnp.bfloat16)
    ret = yo.reshape(epd, ndev, cap, d).transpose(1, 0, 2, 3).reshape(nexp * cap, d)
    back = lax.all_to_all(ret, ('b', 'cp'), 0, 0, tiled=True)
    return combine(back[idx], gate, ffn, u)


def solution(mesh):
    ncp = mesh.shape['cp']
    ndev = mesh.shape['b'] * ncp
    tok = P(('dp', 'b'), 'cp', None)
    rep = P()
    exs = P(('b', 'cp'), None, None)

    def body(x, ids, g_attn, wq, wk, wv, wo, g_ffn, w1, w3, w2, g_moe, wr, we_g, we_u, we_d):
        bd, sd, d = x.shape
        nh = wq.shape[1] // HEAD
        kvh = wk.shape[1] // HEAD
        grp = nh // kvh
        ci = lax.axis_index('cp')
        pos = ci * sd + jnp.arange(sd)
        n = rms_norm(x, g_attn)
        q = rope(proj(n, wq).reshape(bd, sd, nh, HEAD), pos).reshape(bd, sd, kvh, grp, HEAD).transpose(0, 2, 3, 1, 4)
        kv = jnp.stack([rope(proj(n, wk).reshape(bd, sd, kvh, HEAD), pos), proj(n, wv).reshape(bd, sd, kvh, HEAD)])
        mx = jnp.full((bd, kvh, grp, sd), -1e30, jnp.float32)
        den = jnp.zeros((bd, kvh, grp, sd), jnp.float32)
        acc = jnp.zeros((bd, kvh, grp, sd, HEAD), jnp.float32)
        mx, den, acc = attend(q, kv[0], kv[1], pos, pos, mx, den, acc)
        perm = [(j, (j + 1) % ncp) for j in range(ncp)]
        for step in range(1, ncp):
            kv = lax.ppermute(kv, 'cp', perm)
            kpos = ((ci - step) % ncp) * sd + jnp.arange(sd)
            mx, den, acc = attend(q, kv[0], kv[1], pos, kpos, mx, den, acc)
        o = (acc / den[..., None]).astype(jnp.bfloat16).transpose(0, 3, 1, 2, 4).reshape(bd, sd, nh * HEAD)
        y = (x.astype(jnp.float32) + proj(o, wo).astype(jnp.float32)).astype(jnp.bfloat16)
        f = swiglu(rms_norm(y, g_ffn), w1, w3, w2)
        m = moe(rms_norm(x, g_moe).reshape(bd * sd, d), ids, wr, we_g, we_u, we_d, ndev)
        h = y.astype(jnp.float32) + f.astype(jnp.float32) + m.reshape(bd, sd, d)
        return h.astype(jnp.bfloat16)

    return jax.shard_map(body, mesh=mesh, in_specs=(tok, tok, rep, rep, rep, rep, rep, rep, rep, rep, rep, rep, rep, exs, exs, exs), out_specs=tok, check_vma=False)
```

profile of v0, /device:TPU:24, one launch (start us, length us, event | category | flops | bytes accessed | tf_op | source)
XLA Modules:
  0.0 1418.5 jit_solution(15795382874576645039)
XLA Ops:
  5.2 19.0 %convolution_convert_fusion.1 = bf16[64,96,2048]{2,1,0:T(8,128)(2,1)} fusion(f32[64,512]{1,0:T(8,128)S(1)} %get-tuple-element.40, f32[64,512]{1,0:T(8,128)S(1)} %bitcast.181, bf16[1,512,2048]{2,1,0:T(8,128)(2,1)} %param.16, f32[2048]{0:T(1024)S(1)} %convert_element_type.217, f32[512]{0:T(512)S(1)} %add_rsqrt_fusion.1), kind=kOutput, calls=%fused_computation.17 | convolution fusion | flops 12911116288 | bytes 27535360 | tf_op jit(solution)/shard_map/ect,td->ecd/dot_general | solution.py:75
  24.3 546.5 %all_to_all.21 = bf16[16,384,2048]{2,1,0:T(8,128)(2,1)S(1)} all-to-all(bf16[16,384,2048]{2,1,0:T(8,128)(2,1)} %bitcast.167), channel_id=1, replica_groups=mesh['dp'=2,'b'=4,'cp'=4] {'b','cp'}, dimensions={0} | all-to-all | bytes 50331648 | tf_op jit(solution)/shard_map/all_to_all | solution.py:92
  570.8 10.6 copy.80
  581.5 32.1 %fusion.113 = f32[4,1536,1024]{2,1,0:T(8,128)} fusion(bf16[4,1536,2048]{2,1,0:T(8,128)(2,1)} %bitcast.165, bf16[4,2048,1024]{2,1,0:T(8,128)(2,1)S(1)} %bitcast.183), kind=kOutput, calls=%fused_computation.175 | convolution fusion | flops 25769803776 | bytes 67108864 | tf_op jit(solution)/shard_map/ecd,edf->ecf/dot_general | solution.py:94
  613.6 39.1 %multiply_convert_fusion.clone.4 = bf16[4,1536,1024]{2,1,0:T(8,128)(2,1)} fusion(f32[4,1536,1024]{2,1,0:T(8,128)} %fusion.113, bf16[4,1536,2048]{2,1,0:T(8,128)(2,1)} %bitcast.166, bf16[4,2048,1024]{2,1,0:T(8,128)(2,1)} %param.30), kind=kOutput, calls=%fused_computation.3.clone.clone.clone.1 | convolution fusion | flops 25807552512 | bytes 79691776 | tf_op jit(solution)/shard_map/ecd,edf->ecf/dot_general | solution.py:95
  652.7 36.3 %convolution_convert_fusion = bf16[4,1536,2048]{2,1,0:T(8,128)(2,1)} fusion(bf16[4,1024,2048]{2,1,0:T(8,128)(2,1)} %param.31, bf16[4,1536,1024]{2,1,0:T(8,128)(2,1)} %multiply_convert_fusion.clone.4), kind=kOutput, calls=%fused_computation.2 | convolution fusion | flops 25782386688 | bytes 54525952 | tf_op jit(solution)/shard_map/ecf,efd->ecd/dot_general | solution.py:97
  689.1 21.0 %copy.81 = bf16[4,16,96,2048]{3,2,0,1:T(8,128)(2,1)} copy(bf16[4,16,96,2048]{3,2,1,0:T(8,128)(2,1)} %bitcast.168) | data formatting | bytes 50331648 | tf_op jit(solution)/shard_map/reshape | solution.py:98
  710.1 8.5 all-to-all-start.1
  718.7 8.3 fusion.80
  728.9 7.1 convert_bitcast_fusion
  769.4 165.7 %collective-permute-done = bf16[2,1,512,16,128]{4,2,3,1,0:T(8,128)(2,1)} collective-permute-done((bf16[2,1,512,16,128]{4,2,3,1,0:T(8,128)(2,1)S(1)}, bf16[2,1,512,16,128]{4,2,3,1,0:T(8,128)(2,1)}, u32[]{:S(2)}, u32[]{:S(2)}) %collective-permute-start) | collective-permute-done | bytes 4194336 | tf_op jit(solution)/shard_map/ppermute | solution.py:126
  936.8 79.5 %collective-permute-done.1 = bf16[2,1,512,16,128]{4,2,3,1,0:T(8,128)(2,1)} collective-permute-done((bf16[2,1,512,16,128]{4,2,3,1,0:T(8,128)(2,1)}, bf16[2,1,512,16,128]{4,2,3,1,0:T(8,128)(2,1)}, u32[]{:S(2)}, u32[]{:S(2)}) %collective-permute-start.1) | collective-permute-done | bytes 4194336 | tf_op jit(solution)/shard_map/ppermute | solution.py:126
  1026.9 8.1 fusion
  1035.0 8.8 fusion.1
  1043.8 8.9 fusion.2
  1052.7 45.2 %collective-permute-done.2 = bf16[2,1,512,16,128]{4,2,3,1,0:T(8,128)(2,1)} collective-permute-done((bf16[2,1,512,16,128]{4,2,3,1,0:T(8,128)(2,1)}, bf16[2,1,512,16,128]{4,2,3,1,0:T(8,128)(2,1)}, u32[]{:S(2)}, u32[]{:S(2)}) %collective-permute-start.2) | collective-permute-done | bytes 4194336 | tf_op jit(solution)/shard_map/ppermute | solution.py:126
  1097.9 8.9 fusion.3
  1106.9 9.2 fusion.10
  1116.1 9.2 fusion.8
  1125.3 9.2 fusion.6
  1134.5 9.5 fusion.4
  1144.7 12.1 fusion.21
  1156.8 12.4 fusion.17
  1169.3 12.8 fusion.19
  1182.1 12.9 divide_convert_fusion
  1195.1 8.5 fusion.47
  1203.6 27.1 %fusion.59 = f32[512,8192]{1,0:T(8,128)} fusion(bf16[2048,8192]{1,0:T(8,128)(2,1)} %param.24, bf16[1,512,2048]{2,1,0:T(8,128)(2,1)S(1)} %get-tuple-element.43, f32[2048]{0:T(1024)S(1)} %convert_element_type.211, f32[512]{0:T(512)S(1)} %add_rsqrt_fusion), kind=kOutput, calls=%fused_computation.89 | convolution fusion | flops 17184063488 | bytes 52439040 | tf_op jit(solution)/shard_map/dot_general | solution.py:37
  1230.6 31.7 %multiply_convert_fusion.1.clone.8 = bf16[512,8192]{1,0:T(8,128)(2,1)} fusion(f32[512,8192]{1,0:T(8,128)} %fusion.59, bf16[2048,8192]{1,0:T(8,128)(2,1)} %param.25, bf16[1,512,2048]{2,1,0:T(8,128)(2,1)S(1)} %get-tuple-element.43, f32[2048]{0:T(1024)S(1)} %convert_element_type.211, f32[512]{0:T(512)S(1)} %add_rsqrt_fusion), kind=kOutput, calls=%fused_computation.4.clone.clone.clone.clone.clone.clone.clone.1 | convolution fusion | flops 17209229312 | bytes 60827648 | tf_op jit(solution)/shard_map/dot_general | solution.py:37
  1262.4 57.8 %gather_fusion = bf16[6144,2048]{1,0:T(8,128)(2,1)} fusion(bf16[6144,2048]{1,0:T(8,128)(2,1)} %bitcast.39, s32[6144]{0:T(1024)S(1)} %copy-done.16), kind=kCustom, calls=%fused_computation | custom fusion | bytes 50356224 | tf_op jit(solution)/shard_map/gather | solution.py:100
  1320.2 42.0 %reshape.727 = f32[512,12,2048]{2,1,0:T(8,128)} reshape(bf16[6144,2048]{1,0:T(8,128)(2,1)} %gather_fusion) | data formatting | bytes 75497472 | tf_op jit(solution)/shard_map/convert_element_type | solution.py:79
  1362.2 31.4 %multiply_reduce_fusion = f32[512,2048]{1,0:T(8,128)S(1)} fusion(f32[512,12,2048]{2,1,0:T(8,128)} %reshape.727, f32[512,2048]{1,0:T(8,128)} %bitcast_convert_fusion, f32[512,12]{1,0:T(8,128)S(1)} %copy-done.19, pred[512,12]{1,0:T(8,128)(4,1)S(1)} %copy-done.24), kind=kLoop, calls=%fused_computation.1 | loop fusion | flops 36700160 | bytes 58750976 | tf_op jit(solution)/shard_map/reduce_sum | solution.py:80
  1393.6 24.7 %fusion.51 = bf16[1,512,2048]{2,1,0:T(8,128)(2,1)} fusion(bf16[1,512,2048]{2,1,0:T(8,128)(2,1)S(1)} %get-tuple-element.43, f32[512,2048]{1,0:T(8,128)S(1)} %multiply_reduce_fusion, bf16[8192,2048]{1,0:T(8,128)(2,1)} %param.26, bf16[512,8192]{1,0:T(8,128)(2,1)} %multiply_convert_fusion.1.clone.8), kind=kOutput, calls=%fused_computation.68 | convolution fusion | flops 17186160640 | bytes 50331648 | tf_op jit(solution)/shard_map/dot_general | solution.py:33
  (133 shorter events, 53.2 us)
Async XLA Ops:
  0.0 935.0 %copy-start = (bf16[2048,96]{0,1:T(8,128)(2,1)S(1)}, bf16[2048,96]{0,1:T(8,128)(2,1)}, u32[]{:S(2)}) copy-start(bf16[2048,96]{0,1:T(8,128)(2,1)} %param.28) | copy-start | bytes 1179652
  2.1 22.1 %copy-start.30 = (f32[512]{0:T(512)}, f32[512]{0:T(512)S(1)}, u32[]{:S(2)}) copy-start(f32[512]{0:T(512)S(1)} %add_rsqrt_fusion.1) | copy-start | bytes 6148
  4.5 19.8 %copy-start.22 = (f32[512,64]{0,1:T(8,128)}, f32[512,64]{0,1:T(8,128)S(1)}, u32[]{:S(2)}) copy-start(f32[512,64]{0,1:T(8,128)S(1)} %get-tuple-element.41) | copy-start | bytes 393220
  5.2 19.1 %copy-start.26 = (f32[2048]{0:T(1024)}, f32[2048]{0:T(1024)S(1)}, u32[]{:S(2)}) copy-start(f32[2048]{0:T(1024)S(1)} %convert_element_type.217) | copy-start | bytes 24580
  24.3 557.1 %slice-start = ((s8[16777216]{0:T(1024)(128)(4,1)}), s8[4194304]{0:T(1024)(128)(4,1)S(1)}, s32[]{:S(2)}) async-start(s8[16777216]{0:T(1024)(128)(4,1)} %bitcast.182), calls=%async_computation.2 | async-start | bytes 8388608
  24.3 557.1 %slice-start.1 = ((s8[16777216]{0:T(1024)(128)(4,1)}), s8[4194304]{0:T(1024)(128)(4,1)S(1)}, s32[]{:S(2)}) async-start(s8[16777216]{0:T(1024)(128)(4,1)} %bitcast.182), calls=%async_computation.3 | async-start | bytes 8388608
  570.8 10.7 slice-start.2
  570.8 10.7 slice-start.3
  710.1 8.5 copy-start.32
  710.1 8.5 copy-start.7
  710.1 8.6 copy-start.31
  710.1 552.3 %all-to-all-start.1 = ((bf16[16,384,2048]{2,1,0:T(8,128)(2,1)}), bf16[16,384,2048]{2,1,0:T(8,128)(2,1)}, u32[]{:S(2)}, u32[]{:S(2)}) async-start(bf16[16,384,2048]{2,1,0:T(8,128)(2,1)} %bitcast.161), calls=%async_computation.1 | async-start | bytes 50331648 | tf_op jit(solution)/shard_map/all_to_all | solution.py:99
  727.0 12.1 slice-start.4
  728.9 10.1 slice-start.5
  767.1 168.0 %copy-start.8 = (bf16[1,512,2048]{2,1,0:T(8,128)(2,1)S(1)}, bf16[1,512,2048]{2,1,0:T(8,128)(2,1)}, u32[]{:S(2)}) copy-start(bf16[1,512,2048]{2,1,0:T(8,128)(2,1)} %param.16) | copy-start | bytes 6291460
  767.1 167.9 %copy-start.27 = (f32[2048]{0:T(1024)S(1)}, f32[2048]{0:T(1024)}, u32[]{:S(2)}) copy-start(f32[2048]{0:T(1024)} %copy-done.26) | copy-start | bytes 24580
  769.2 166.8 %copy-start.21 = (s32[1,512,12]{1,2,0:T(8,128)S(1)}, s32[1,512,12]{1,2,0:T(8,128)}, u32[]{:S(2)}) copy-start(s32[1,512,12]{1,2,0:T(8,128)} %copy-done.20) | copy-start | bytes 73732
  769.2 167.3 %copy-start.18 = (pred[512,12,96]{0,2,1:T(8,128)(4,1)S(1)}, pred[512,12,96]{0,2,1:T(8,128)(4,1)}, u32[]{:S(2)}) copy-start(pred[512,12,96]{0,2,1:T(8,128)(4,1)} %copy-done.17) | copy-start | bytes 1769476
  769.2 167.3 %copy-start.23 = (f32[512,64]{0,1:T(8,128)S(1)}, f32[512,64]{0,1:T(8,128)}, u32[]{:S(2)}) copy-start(f32[512,64]{0,1:T(8,128)} %copy-done.22) | copy-start | bytes 393220
  769.2 167.6 %copy-start.25 = (s32[1,512,12]{1,0,2:T(1,128)S(1)}, s32[1,512,12]{1,0,2:T(1,128)}, u32[]{:S(2)}) copy-start(s32[1,512,12]{1,0,2:T(1,128)} %param.17) | copy-start | bytes 73732
  769.2 249.1 %copy-start.33 = (bf16[2048]{0:T(1024)(128)(2,1)S(1)}, bf16[2048]{0:T(1024)(128)(2,1)}, u32[]{:S(2)}) copy-start(bf16[2048]{0:T(1024)(128)(2,1)} %param.23) | copy-start | bytes 12292
  769.2 165.8 %collective-permute-start = (bf16[2,1,512,16,128]{4,2,3,1,0:T(8,128)(2,1)S(1)}, bf16[2,1,512,16,128]{4,2,3,1,0:T(8,128)(2,1)}, u32[]{:S(2)}, u32[]{:S(2)}) collective-permute-start(bf16[2,1,512,16,128]{4,2,3,1,0:T(8,128)(2,1)S(1)} %pad_maximum_fusion), channel_id=1, source_target_pairs={{0,1},{1,2},{2,3},{3,0},{4,5},{5,6},{6,7},{7,4},{8,9},{9,10},{10,1... | collective-permute-start | bytes 12582920 | tf_op jit(solution)/shard_map/ppermute | solution.py:126
  935.0 81.3 %collective-permute-start.1 = (bf16[2,1,512,16,128]{4,2,3,1,0:T(8,128)(2,1)}, bf16[2,1,512,16,128]{4,2,3,1,0:T(8,128)(2,1)}, u32[]{:S(2)}, u32[]{:S(2)}) collective-permute-start(bf16[2,1,512,16,128]{4,2,3,1,0:T(8,128)(2,1)} %collective-permute-done), channel_id=1, source_target_pairs={{0,1},{1,2},{2,3},{3,0},{4,5},{5,6},{6,7},{7,4},{8,9},{9,10},{10,1... | collective-permute-start | bytes 12582920 | tf_op jit(solution)/shard_map/ppermute | solution.py:126
  1016.3 81.6 %collective-permute-start.2 = (bf16[2,1,512,16,128]{4,2,3,1,0:T(8,128)(2,1)}, bf16[2,1,512,16,128]{4,2,3,1,0:T(8,128)(2,1)}, u32[]{:S(2)}, u32[]{:S(2)}) collective-permute-start(bf16[2,1,512,16,128]{4,2,3,1,0:T(8,128)(2,1)} %collective-permute-done.1), channel_id=1, source_target_pairs={{0,1},{1,2},{2,3},{3,0},{4,5},{5,6},{6,7},{7,4},{8,9},{9,10},{10,1... | collective-permute-start | bytes 12582920 | tf_op jit(solution)/shard_map/ppermute | solution.py:126
  1134.5 10.2 copy-start.12
  1169.3 12.8 copy-start.28
  1169.3 12.8 copy-start.29
  1182.1 13.0 copy-start.10
  1230.6 31.7 %copy-start.16 = (s32[6144]{0:T(1024)S(1)}, s32[6144]{0:T(1024)}, u32[]{:S(2)}) copy-start(s32[6144]{0:T(1024)} %broadcast_clamp_fusion) | copy-start | bytes 73732
  1320.2 42.0 %copy-start.19 = (f32[512,12]{1,0:T(8,128)S(1)}, f32[512,12]{1,0:T(8,128)}, u32[]{:S(2)}) copy-start(f32[512,12]{1,0:T(8,128)} %copy.78) | copy-start | bytes 73732
  1320.2 42.0 %copy-start.24 = (pred[512,12]{1,0:T(8,128)(4,1)S(1)}, pred[512,12]{1,0:T(8,128)(4,1)}, u32[]{:S(2)}) copy-start(pred[512,12]{1,0:T(8,128)(4,1)} %copy.79) | copy-start | bytes 18436
  1393.6 24.7 %copy-start.1 = (bf16[2048,96]{0,1:T(8,128)(2,1)S(1)}, bf16[2048,96]{0,1:T(8,128)(2,1)}, u32[]{:S(2)}) copy-start(bf16[2048,96]{0,1:T(8,128)(2,1)} %param.28) | copy-start | bytes 1179652
  (12 other events, 41.4 us)
where the time goes:
time: 1430 us; the launch traced here: 1420 us
  blocking collectives  546 us (38%)
  matrix products  326 us (23%)
  waiting for transfers between devices  290 us (20%)
  local copies, waits for them, and re-layouts  154 us (11%)
  other arithmetic  91.7 us (6%)
    all_to_all x1, blocking collectives, moe(): recv = lax.all_to_all(send, ('b', 'cp'), 0, 0, tiled=True)  546 us
    ppermute x3, waiting for transfers between devices, body(): kv = lax.ppermute(kv, 'cp', perm)  290 us
    gather x1, local copies, waits for them, and re-layouts, moe(): return combine(back[idx], gate, ffn, u)  57.8 us
    dot_general x5, matrix products, proj(): jnp.dot(a, wt, preferred_element_type=jnp.float32).astype(jnp.bfloat16)  54.3 us
    dot_general x4, matrix products, attend(): jnp.einsum('bkgqs,bskd->bkgqd', p.astype(jnp.bfloat16), vb, preferred_ele...  50.4 us
    convert_element_type x1, local copies, waits for them, and re-layouts, combine(): got.astype(jnp.float32)  42 us
    dot_general x1, matrix products, moe(): jnp.einsum('ecd,edf->ecf', xin, we_u, preferred_element_type=jnp.float32)  39.1 us
    reduce_sum x4, other arithmetic, attend(): den = den * corr + jnp.sum(p, axis=-1)  37.1 us
  transfers between devices with their start and end apart: 4, of which 3 were waited for; matrix products, arithmetic and copies ran while one was open for 18% of the time, Pallas kernels for 0%

commit v1 on v0

v1 whole, which is shorter than its diff:
```python
import jax
import jax.numpy as jnp
from jax import lax
from jax.sharding import PartitionSpec as P

HEAD = 128
ROPE = 64
EPS = 1e-6
THETA = 10000.0
RSCALE = 2.5


def rms_norm(x, g):
    xf = x.astype(jnp.float32)
    r = lax.rsqrt(jnp.mean(xf * xf, axis=-1, keepdims=True) + EPS)
    return (xf * r * g.astype(jnp.float32)).astype(jnp.bfloat16)


def rope(t, pos):
    half = ROPE // 2
    freq = THETA ** (-jnp.arange(half, dtype=jnp.float32) / half)
    ang = pos.astype(jnp.float32)[:, None] * freq[None, :]
    c = jnp.cos(ang)[:, None, :]
    s = jnp.sin(ang)[:, None, :]
    tf = t.astype(jnp.float32)
    t1 = tf[..., :half]
    t2 = tf[..., half:ROPE]
    out = jnp.concatenate([t1 * c - t2 * s, t2 * c + t1 * s, tf[..., ROPE:]], axis=-1)
    return out.astype(jnp.bfloat16)


def proj(a, wt):
    return jnp.dot(a, wt, preferred_element_type=jnp.float32).astype(jnp.bfloat16)


def swiglu(z, wa, wb, wc):
    hh = (jax.nn.silu(jnp.dot(z, wa, preferred_element_type=jnp.float32)) * jnp.dot(z, wb, preferred_element_type=jnp.float32)).astype(jnp.bfloat16)
    return proj(hh, wc)


def attend(q, kb, vb, qpos, kpos, mx, den, acc):
    s = jnp.einsum('bkgqd,bskd->bkgqs', q, kb, preferred_element_type=jnp.float32) * (HEAD ** -0.5)
    s = jnp.where(qpos[:, None] >= kpos[None, :], s, -1e30)
    mnew = jnp.maximum(mx, jnp.max(s, axis=-1))
    corr = jnp.exp(mx - mnew)
    p = jnp.exp(s - mnew[..., None])
    den = den * corr + jnp.sum(p, axis=-1)
    pv = jnp.einsum('bkgqs,bskd->bkgqd', p.astype(jnp.bfloat16), vb, preferred_element_type=jnp.float32)
    acc = acc * corr[..., None] + pv
    return mnew, den, acc


CAP = 96


def gates(u, ids, wr, nexp):
    t = u.shape[0]
    top = ids.shape[-1]
    logits = jnp.dot(u, wr, preferred_element_type=jnp.float32)
    idf = ids.reshape(t, top)
    cols = jnp.arange(logits.shape[1])
    pick = idf[:, :, None] == cols[None, None, :]
    gate = RSCALE * jax.nn.softmax(jnp.sum(jnp.where(pick, logits[:, None, :], 0.0), axis=-1), axis=-1)
    gsum = jnp.sum(jnp.where(pick, gate[..., None], 0.0), axis=1)
    have = jnp.any(pick, axis=1)
    zero = jnp.sum(gsum[:, nexp:], axis=-1, keepdims=True)
    table = jnp.where(have, gsum, -1.0)[:, :nexp]
    return table.T, zero


def split3(g):
    hi = g.astype(jnp.bfloat16)
    r = g - hi.astype(jnp.float32)
    mid = r.astype(jnp.bfloat16)
    lo = (r - mid.astype(jnp.float32)).astype(jnp.bfloat16)
    return hi, mid, lo


def moe_partials(uall, tab, we_g, we_u, we_d, nchunk):
    ndev, t, d = uall.shape
    epd = we_g.shape[0]
    have = tab >= 0.0
    ti = jnp.arange(t)
    lower = (ti[:, None] < ti[None, :]).astype(jnp.bfloat16)
    rank = jnp.einsum('set,tr->ser', have.astype(jnp.bfloat16), lower, preferred_element_type=jnp.float32)
    rank = jnp.where(have, rank, -1.0)
    sel = rank[:, :, None, :] == jnp.arange(CAP, dtype=jnp.float32)[None, None, :, None]
    selb = sel.astype(jnp.bfloat16).reshape(ndev, epd * CAP, t)
    xin = jnp.einsum('sct,std->scd', selb, uall, preferred_element_type=jnp.float32).astype(jnp.bfloat16)
    xin = xin.reshape(ndev, epd, CAP, d).transpose(1, 0, 2, 3).reshape(epd, ndev * CAP, d)
    hg = jnp.einsum('ecd,edf->ecf', xin, we_g, preferred_element_type=jnp.float32)
    hu = jnp.einsum('ecd,edf->ecf', xin, we_u, preferred_element_type=jnp.float32)
    hh = (jax.nn.silu(hg) * hu).astype(jnp.bfloat16)
    parts = [jnp.where(sel, p[:, :, None, :], jnp.zeros((), jnp.bfloat16)).reshape(ndev, epd * CAP, t) for p in split3(tab)]
    comb = jnp.concatenate(parts, axis=1)
    outs = []
    w = d // nchunk
    for i in range(nchunk):
        yo = jnp.einsum('ecf,efd->ecd', hh, we_d[:, :, i * w:(i + 1) * w], preferred_element_type=jnp.float32).astype(jnp.bfloat16)
        yo = yo.reshape(epd, ndev, CAP, w).transpose(1, 0, 2, 3).reshape(ndev, epd * CAP, w)
        y3 = jnp.concatenate([yo, yo, yo], axis=1)
        part = jnp.einsum('sct,scd->std', comb, y3, preferred_element_type=jnp.float32)
        outs.append(part.reshape(ndev * t, w))
    return outs


NCHUNK = 2


def solution(mesh):
    ncp = mesh.shape['cp']
    ndev = mesh.shape['b'] * ncp
    tok = P(('dp', 'b'), 'cp', None)
    rep = P()
    exs = P(('b', 'cp'), None, None)

    def body(x, ids, g_attn, wq, wk, wv, wo, g_ffn, w1, w3, w2, g_moe, wr, we_g, we_u, we_d):
        bd, sd, d = x.shape
        nh = wq.shape[1] // HEAD
        nexp = we_g.shape[0] * ndev
        u = rms_norm(x, g_moe).reshape(bd * sd, d)
        uall = lax.all_gather(u, ('b', 'cp'), axis=0, tiled=False)
        tab, zero = gates(u, ids, wr, nexp)
        tall = lax.all_gather(tab, ('b', 'cp'), axis=0, tiled=False)
        ci = lax.axis_index('cp')
        epd = we_g.shape[0]
        e0 = (lax.axis_index('b') * ncp + ci) * epd
        tall = lax.dynamic_slice_in_dim(tall, e0, epd, axis=1)
        pos = ci * sd + jnp.arange(sd)
        n = rms_norm(x, g_attn)
        q = rope(proj(n, wq).reshape(bd, sd, nh, HEAD), pos).reshape(bd, sd, nh, 1, HEAD).transpose(0, 2, 3, 1, 4)
        kv = jnp.stack([rope(proj(n, wk).reshape(bd, sd, nh, HEAD), pos), proj(n, wv).reshape(bd, sd, nh, HEAD)])
        mx = jnp.full((bd, nh, 1, sd), -1e30, jnp.float32)
        den = jnp.zeros((bd, nh, 1, sd), jnp.float32)
        acc = jnp.zeros((bd, nh, 1, sd, HEAD), jnp.float32)
        mx, den, acc = attend(q, kv[0], kv[1], pos, pos, mx, den, acc)
        for step in range(1, ncp):
            kv = lax.ppermute(kv, 'cp', [(j, j + 1) for j in range(step - 1, ncp - 1)])
            kpos = ((ci - step) % ncp) * sd + jnp.arange(sd)
            mx, den, acc = attend(q, kv[0], kv[1], pos, kpos, mx, den, acc)
        o = (acc / den[..., None]).astype(jnp.bfloat16).transpose(0, 3, 1, 2, 4).reshape(bd, sd, nh * HEAD)
        y = (x.astype(jnp.float32) + proj(o, wo).astype(jnp.float32)).astype(jnp.bfloat16)
        parts = moe_partials(uall, tall, we_g, we_u, we_d, NCHUNK)
        y, parts = lax.optimization_barrier((y, parts))
        ms = [lax.psum_scatter(p, ('b', 'cp'), scatter_dimension=0, tiled=True) for p in parts]
        f = swiglu(rms_norm(y, g_ffn), w1, w3, w2)
        base = y.astype(jnp.float32) + f.astype(jnp.float32)
        m = jnp.concatenate(ms, axis=1) + zero * u.astype(jnp.float32)
        h = base + m.reshape(bd, sd, d)
        return h.astype(jnp.bfloat16)

    return jax.shard_map(body, mesh=mesh, in_specs=(tok, tok, rep, rep, rep, rep, rep, rep, rep, rep, rep, rep, rep, exs, exs, exs), out_specs=tok, check_vma=False)
```

time: 1430 us -> 1490 us (1.042)
  blocking collectives: 546 us -> 0 us
  waiting for transfers between devices: 290 us -> 830 us
  matrix products: 326 us -> 429 us
  local copies, waits for them, and re-layouts: 154 us -> 113 us
    reduce_scatter x0 -> x2, waiting for transfers between devices: none -> 823 us  [body(): lax.psum_scatter(p, ('b', 'cp'), scatter_dimension=0, tiled=True)]
    all_to_all x1 -> x0, blocking collectives: 546 us -> none  [moe(): recv = lax.all_to_all(send, ('b', 'cp'), 0, 0, tiled=True)]
    ppermute x3, waiting for transfers between devices: 290 us -> 5.42 us  [body(): kv = lax.ppermute(kv, 'cp', [(j, j + 1) for j in range(step - 1, ncp - 1)])]
    dot_general x6 -> x9, matrix products: 128 us -> 231 us  [the longest x2 82 us: moe_partials(): jnp.einsum('sct,scd->std', comb, y3, preferred_element_type=jnp.float32)]
    gather x1 -> x0, local copies, waits for them, and re-layouts: 57.8 us -> none  [moe(): return combine(back[idx], gate, ffn, u)]
    convert_element_type x1 -> x3, local copies, waits for them, and re-layouts: 42 us -> 0.16 us  [the longest x1 0.05 us: split3(): hi = g.astype(jnp.bfloat16)]
    transpose x0 -> x3, local copies, waits for them, and re-layouts: none -> 37.7 us  [the longest x1 21 us: moe_partials(): xin.reshape(ndev, epd, CAP, d).transpose(1, 0, 2, 3)]
    broadcast_in_dim x0 -> x6, local copies, waits for them, and re-layouts: none -> 35.4 us  [moe_partials(): jnp.where(sel, p[:, :, None, :], jnp.zeros((), jnp.bfloat16))]
  transfers between devices with their start and end apart: 4 -> 7, of which waited for: 3 -> 3; matrix products, arithmetic and copies ran while one was open for 18% -> 22% of each run, Pallas kernels for 0% -> 0%
where the time goes in v1:
time: 1490 us; the launch traced here: 1480 us
  waiting for transfers between devices  830 us (56%)
  matrix products  429 us (29%)
  local copies, waits for them, and re-layouts  113 us (8%)
  other arithmetic  82.9 us (6%)
    reduce_scatter x2, waiting for transfers between devices, body(): lax.psum_scatter(p, ('b', 'cp'), scatter_dimension=0, tiled=True)  823 us
    dot_general x2, matrix products, moe_partials(): jnp.einsum('sct,scd->std', comb, y3, preferred_element_type=jnp.float32)  82 us
    dot_general x5, matrix products, proj(): jnp.dot(a, wt, preferred_element_type=jnp.float32).astype(jnp.bfloat16)  58.4 us
    dot_general x4, matrix products, attend(): jnp.einsum('bkgqs,bskd->bkgqd', p.astype(jnp.bfloat16), vb, preferred_ele...  51.3 us
    dot_general x2, matrix products, moe_partials(): jnp.einsum('ecf,efd->ecd', hh, we_d[:, :, i * w:(i + 1) * w], preferred_e...  42.6 us
    dot_general x1, matrix products, moe_partials(): jnp.einsum('ecd,edf->ecf', xin, we_u, preferred_element_type=jnp.float32)  39.2 us
    reduce_sum x4, other arithmetic, attend(): den = den * corr + jnp.sum(p, axis=-1)  37.1 us
    dot_general x1, matrix products, moe_partials(): jnp.einsum('ecd,edf->ecf', xin, we_g, preferred_element_type=jnp.float32)  36.2 us
  transfers between devices with their start and end apart: 7, of which 3 were waited for; matrix products, arithmetic and copies ran while one was open for 22% of the time, Pallas kernels for 0%

profile of v1, /device:TPU:24, one launch (start us, length us, event | category | flops | bytes accessed | tf_op | source)
XLA Modules:
  0.0 1477.9 jit_solution(9683946366072923837)
XLA Ops:
  15.7 8.7 fusion.79
  100.1 8.9 copy.119
  115.2 12.6 copy.117
  142.7 8.7 copy.123
  151.4 10.8 broadcast_select_fusion.2
  162.2 8.9 broadcast_select_fusion.1
  171.1 8.8 fusion.13
  179.9 8.9 fusion.14
  188.8 9.2 fusion.15
  198.0 9.2 fusion.22
  207.2 9.2 fusion.20
  216.4 9.2 fusion.18
  225.6 9.5 fusion.16
  235.7 12.1 fusion.30
  247.9 12.6 fusion.26
  260.4 12.7 fusion.28
  273.2 13.9 divide_convert_fusion
  287.1 10.1 fusion.55
  297.2 29.7 %convolution_convert_fusion.2 = bf16[16,384,2048]{2,1,0:T(8,128)(2,1)} fusion(pred[16,384,512]{1,2,0:T(32,128)(4,1)S(1)} %copy-done.13, bf16[16,512,2048]{2,1,0:T(8,128)(2,1)} %all-gather.4.cloned.1.call-done), kind=kOutput, calls=%fused_computation.29 | convolution fusion | flops 12897484800 | bytes 61865984 | tf_op jit(solution)/shard_map/sct,std->scd/dot_general | solution.py:89
  326.9 21.0 %copy.125 = bf16[4,16,96,2048]{3,2,1,0:T(8,128)(2,1)} copy(bf16[4,16,96,2048]{3,2,0,1:T(8,128)(2,1)} %bitcast.148) | data formatting | bytes 50331648 | tf_op jit(solution)/shard_map/transpose | solution.py:90
  347.9 36.2 %fusion.117 = f32[4,1536,1024]{2,1,0:T(8,128)} fusion(bf16[4,1536,2048]{2,1,0:T(8,128)(2,1)} %bitcast.149, bf16[4,2048,1024]{2,1,0:T(8,128)(2,1)} %param.29), kind=kOutput, calls=%fused_computation.183 | convolution fusion | flops 25769803776 | bytes 67108864 | tf_op jit(solution)/shard_map/ecd,edf->ecf/dot_general | solution.py:91
  384.1 39.2 %multiply_convert_fusion = bf16[4,1536,1024]{2,1,0:T(8,128)(2,1)} fusion(f32[4,1536,1024]{2,1,0:T(8,128)} %fusion.117, bf16[4,1536,2048]{2,1,0:T(8,128)(2,1)} %bitcast.150, bf16[4,2048,1024]{2,1,0:T(8,128)(2,1)} %param.30), kind=kOutput, calls=%fused_computation.12 | convolution fusion | flops 25807552512 | bytes 79691776 | tf_op jit(solution)/shard_map/ecd,edf->ecf/dot_general | solution.py:92
  423.3 21.4 %convolution_convert_fusion.1 = bf16[4,1536,1024]{2,1,0:T(8,128)(2,1)} fusion(bf16[4,1536,1024]{2,1,0:T(8,128)(2,1)} %multiply_convert_fusion, bf16[4,1024,2048]{2,1,0:T(8,128)(2,1)} %param.31), kind=kOutput, calls=%fused_computation.28 | convolution fusion | flops 12891193344 | bytes 33554432 | tf_op jit(solution)/shard_map/ecf,efd->ecd/dot_general | solution.py:99
  444.6 21.2 %convolution_convert_fusion = bf16[4,1536,1024]{2,1,0:T(8,128)(2,1)} fusion(bf16[4,1536,1024]{2,1,0:T(8,128)(2,1)} %multiply_convert_fusion, bf16[4,1024,2048]{2,1,0:T(8,128)(2,1)} %param.31), kind=kOutput, calls=%fused_computation.27 | convolution fusion | flops 12891193344 | bytes 33554432 | tf_op jit(solution)/shard_map/ecf,efd->ecd/dot_general | solution.py:99
  465.8 11.5 copy.126
  484.0 41.1 %fusion = f32[16,512,1024]{2,1,0:T(8,128)} fusion(bf16[16,384,1024]{2,1,0:T(8,128)(2,1)} %bitcast.161, bf16[16,384,512]{1,2,0:T(8,128)(2,1)} %get-tuple-element.27, bf16[16,384,512]{1,2,0:T(8,128)(2,1)} %get-tuple-element.26, bf16[16,384,512]{1,2,0:T(8,128)(2,1)} %get-tuple-element.11), kind=kOutput, calls=%fused_computation | convolution fusion | flops 19497222144 | bytes 65011712 | tf_op jit(solution)/shard_map/sct,scd->std/dot_general | solution.py:102
  525.1 40.9 %fusion.6 = f32[16,512,1024]{2,1,0:T(8,128)} fusion(bf16[16,384,1024]{2,1,0:T(8,128)(2,1)} %bitcast.160, bf16[16,384,512]{1,2,0:T(8,128)(2,1)} %get-tuple-element.27, bf16[16,384,512]{1,2,0:T(8,128)(2,1)} %get-tuple-element.26, bf16[16,384,512]{1,2,0:T(8,128)(2,1)} %get-tuple-element.11), kind=kOutput, calls=%fused_computation.6 | convolution fusion | flops 19497222144 | bytes 65011712 | tf_op jit(solution)/shard_map/sct,scd->std/dot_general | solution.py:102
  568.1 26.9 %fusion.88 = f32[512,8192]{1,0:T(8,128)} fusion(bf16[2048,8192]{1,0:T(8,128)(2,1)} %param.24, bf16[1,512,2048]{2,1,0:T(8,128)(2,1)S(1)} %copy-done.20, f32[2048]{0:T(1024)S(1)} %convert_element_type.215, f32[512]{0:T(512)S(1)} %add_rsqrt_fusion), kind=kOutput, calls=%fused_computation.130 | convolution fusion | flops 17184063488 | bytes 52439040 | tf_op jit(solution)/shard_map/dot_general | solution.py:37
  595.0 27.3 %multiply_convert_fusion.1.clone.8 = bf16[512,8192]{1,0:T(8,128)(2,1)} fusion(f32[512,8192]{1,0:T(8,128)} %fusion.88, bf16[2048,8192]{1,0:T(8,128)(2,1)} %param.25, bf16[1,512,2048]{2,1,0:T(8,128)(2,1)} %fusion.55, f32[2048]{0:T(1024)S(1)} %convert_element_type.215, f32[512]{0:T(512)S(1)} %add_rsqrt_fusion), kind=kOutput, calls=%fused_computation.14.clone.clone.clone.clone.clone.clone.clone.1 | convolution fusion | flops 17209229312 | bytes 60827648 | tf_op jit(solution)/shard_map/dot_general | solution.py:37
  622.3 491.0 %reduce-scatter.5.cloned.1.call-done = f32[512,1024]{1,0:T(8,128)} async-done(((f32[8192,1024]{1,0:T(8,128)}), f32[512,1024]{1,0:T(8,128)}) %reduce-scatter.5.cloned.1.call-update) | async-done | bytes 2097168 | tf_op jit(solution)/shard_map/reduce_scatter | solution.py:145
  1113.3 331.9 %reduce-scatter.3.cloned.1.call-done = f32[512,1024]{1,0:T(8,128)} async-done(((f32[8192,1024]{1,0:T(8,128)}), f32[512,1024]{1,0:T(8,128)}) %reduce-scatter.3.cloned.1.call-update) | async-done | bytes 2097168 | tf_op jit(solution)/shard_map/reduce_scatter | solution.py:145
  1445.2 25.9 %fusion.60 = bf16[1,512,2048]{2,1,0:T(8,128)(2,1)} fusion(bf16[1,512,2048]{2,1,0:T(8,128)(2,1)} %fusion.55, f32[1,512,1024]{2,1,0:T(8,128)} %bitcast.173, f32[1,512,1024]{2,1,0:T(8,128)} %bitcast.174, bf16[1,512,2048]{2,1,0:T(8,128)(2,1)S(1)} %copy-done.11, f32[512]{0:T(512)S(1)} %slice_reduce_fusion, bf16[8192,2048]{1,0:T(8,128)(2,1)} %param.26, ...), kind=kOutput, calls=%fused_computation.77 | convolution fusion | flops 17190354944 | bytes 52430848 | tf_op jit(solution)/shard_map/dot_general | solution.py:33
  (130 shorter events, 115.1 us)
Async XLA Ops:
  6.5 6.1 copy-start
  6.5 86.5 %all-gather.6.cloned.1.call-start = ((), (), s32[]{:S(2)}) async-start(), calls=%async_computation.5 | async-start | bytes 2228224 | tf_op jit(solution)/shard_map/all_gather | solution.py:124
  10.4 5.2 copy-start.24
  12.6 2.3 copy-start.10
  14.1 10.3 copy-start.21
  14.8 282.4 %all-gather.4.cloned.1.call-start = ((), (), s32[]{:S(2)}) async-start(), calls=%async_computation.2 | async-start | bytes 35651584 | tf_op jit(solution)/shard_map/all_gather | solution.py:122
  15.6 1097.7 %reduce-scatter.5.cloned.1.call-start = ((), (), s32[]{:S(2)}) async-start(), calls=%async_computation.4 | async-start | bytes 35651584 | tf_op jit(solution)/shard_map/reduce_scatter | solution.py:145
  15.6 10.7 copy-start.15
  24.4 12.8 slice-start
  26.4 10.8 slice-start.1
  45.9 2.6 copy-start.17
  51.8 11.6 copy-start.8
  52.9 3.8 copy-start.2
  58.0 5.4 copy-start.19
  63.4 2.2 copy-start.6
  65.7 9.1 collective-permute-start
  74.8 19.2 %collective-permute-start.1 = (bf16[2,1,512,16,128]{4,2,3,1,0:T(8,128)(2,1)}, bf16[2,1,512,16,128]{4,2,3,1,0:T(8,128)(2,1)}, u32[]{:S(2)}, u32[]{:S(2)}) collective-permute-start(bf16[2,1,512,16,128]{4,2,3,1,0:T(8,128)(2,1)} %collective-permute-done), channel_id=1, source_target_pairs={{1,2},{2,3},{5,6},{6,7},{9,10},{10,11},{13,14},{14,15},{17,18},{18... | collective-permute-start | bytes 12582920 | tf_op jit(solution)/shard_map/ppermute | solution.py:138
  79.8 5.1 copy-start.5
  79.8 5.1 copy-start.7
  79.8 5.1 copy-start.9
  94.0 94.8 %collective-permute-start.2 = (bf16[2,1,512,16,128]{4,2,3,1,0:T(8,128)(2,1)}, bf16[2,1,512,16,128]{4,2,3,1,0:T(8,128)(2,1)}, u32[]{:S(2)}, u32[]{:S(2)}) collective-permute-start(bf16[2,1,512,16,128]{4,2,3,1,0:T(8,128)(2,1)} %collective-permute-done.1), channel_id=1, source_target_pairs={{2,3},{6,7},{10,11},{14,15},{18,19},{22,23},{26,27},{30,31}} | collective-permute-start | bytes 12582920 | tf_op jit(solution)/shard_map/ppermute | solution.py:138
  151.4 10.8 copy-start.3
  162.2 8.9 copy-start.12
  225.6 10.2 copy-start.18
  260.4 12.7 copy-start.22
  260.4 12.7 copy-start.23
  273.2 13.9 copy-start.16
  287.1 10.1 copy-start.13
  465.8 12.9 copy-start.14
  566.0 879.2 %reduce-scatter.3.cloned.1.call-start = ((), (), s32[]{:S(2)}) async-start(), calls=%async_computation.3 | async-start | bytes 35651584 | tf_op jit(solution)/shard_map/reduce_scatter | solution.py:145
  595.0 850.2 %copy-start.11 = (bf16[1,512,2048]{2,1,0:T(8,128)(2,1)S(1)}, bf16[1,512,2048]{2,1,0:T(8,128)(2,1)}, u32[]{:S(2)}) copy-start(bf16[1,512,2048]{2,1,0:T(8,128)(2,1)} %copy-done.10) | copy-start | bytes 6291460
  1445.2 25.9 %copy-start.1 = (bf16[2048,96]{0,1:T(8,128)(2,1)S(1)}, bf16[2048,96]{0,1:T(8,128)(2,1)}, u32[]{:S(2)}) copy-start(bf16[2048,96]{0,1:T(8,128)(2,1)} %param.28) | copy-start | bytes 1179652
  (3 other events, 4.5 us)
Sparse Core Ops, SparseCore 0:
  14.9 41.2 all-gather.5
  57.8 237.7 all-gather.3
  566.1 547.1 reduce-scatter.4
  1117.4 327.7 reduce-scatter.2

commit v2 on v1

v2 whole, which is shorter than its diff:
```python
import jax
import jax.numpy as jnp
from jax import lax
from jax.sharding import PartitionSpec as P


HEAD = 128
ROPE = 64
EPS = 1e-6
THETA = 10000.0
RSCALE = 2.5


def rms_norm(x, g):
    xf = x.astype(jnp.float32)
    r = lax.rsqrt(jnp.mean(xf * xf, axis=-1, keepdims=True) + EPS)
    return (xf * r * g.astype(jnp.float32)).astype(jnp.bfloat16)


def rope(t, pos):
    half = ROPE // 2
    freq = THETA ** (-jnp.arange(half, dtype=jnp.float32) / half)
    ang = pos.astype(jnp.float32)[:, None] * freq[None, :]
    c = jnp.cos(ang)[:, None, :]
    s = jnp.sin(ang)[:, None, :]
    tf = t.astype(jnp.float32)
    t1 = tf[..., :half]
    t2 = tf[..., half:ROPE]
    out = jnp.concatenate([t1 * c - t2 * s, t2 * c + t1 * s, tf[..., ROPE:]], axis=-1)
    return out.astype(jnp.bfloat16)


def proj(a, wt):
    return jnp.dot(a, wt, preferred_element_type=jnp.float32).astype(jnp.bfloat16)


def attend(q, kb, vb, qpos, kpos, mx, den, acc):
    s = jnp.einsum('bkgqd,bskd->bkgqs', q, kb, preferred_element_type=jnp.float32) * (HEAD ** -0.5)
    s = jnp.where(qpos[:, None] >= kpos[None, :], s, -1e30)
    mnew = jnp.maximum(mx, jnp.max(s, axis=-1))
    corr = jnp.exp(mx - mnew)
    p = jnp.exp(s - mnew[..., None])
    den = den * corr + jnp.sum(p, axis=-1)
    pv = jnp.einsum('bkgqs,bskd->bkgqd', p.astype(jnp.bfloat16), vb, preferred_element_type=jnp.float32)
    acc = acc * corr[..., None] + pv
    return mnew, den, acc


CAP = 96
ORDER = ((3, 2, 1, 0), (0, 3, 2, 1), (3, 0, 1, 2), (0, 1, 2, 3))


def gates(u, ids, wr, nexp):
    t = u.shape[0]
    top = ids.shape[-1]
    logits = jnp.dot(u, wr, preferred_element_type=jnp.float32)
    idf = ids.reshape(t, top)
    pick = idf[:, :, None] == jnp.arange(logits.shape[1])[None, None, :]
    gate = RSCALE * jax.nn.softmax(jnp.sum(jnp.where(pick, logits[:, None, :], 0.0), axis=-1), axis=-1)
    zero = jnp.sum(jnp.where(idf >= nexp, gate, 0.0), axis=-1, keepdims=True)
    return jnp.concatenate([idf.astype(jnp.float32), gate], axis=1).T, zero


def tables(info, first, count):
    top = info.shape[1] // 2
    t = info.shape[2]
    ex = (first + jnp.arange(count)).astype(jnp.float32)[None, :, None]
    g = jnp.zeros((info.shape[0], count, t), jnp.float32)
    have = jnp.zeros((info.shape[0], count, t), jnp.bool_)
    for j in range(top):
        hit = info[:, j:j + 1, :] == ex
        g = g + jnp.where(hit, info[:, top + j:top + j + 1, :], 0.0)
        have = have | hit
    ti = jnp.arange(t)
    before = (ti[:, None] < ti[None, :]).astype(jnp.bfloat16)
    rank = jnp.einsum('set,tr->ser', have.astype(jnp.bfloat16), before, preferred_element_type=jnp.float32)
    return g, jnp.where(have, rank, -1.0).astype(jnp.bfloat16)


def split3(g):
    hi = g.astype(jnp.bfloat16)
    r = g - hi.astype(jnp.float32)
    mid = r.astype(jnp.bfloat16)
    lo = (r - mid.astype(jnp.float32)).astype(jnp.bfloat16)
    return hi, mid, lo


def pick_rows(rank):
    epd = rank.shape[1]
    r = jnp.arange(epd * CAP)
    rep = (r[:, None] // CAP == jnp.arange(epd)[None, :]).astype(jnp.bfloat16)
    full = jnp.einsum('re,set->srt', rep, rank, preferred_element_type=jnp.float32)
    return (full == (r % CAP).astype(jnp.float32)[None, :, None]).astype(jnp.bfloat16)


def expert_rows(ublk, sel, we_g, we_u, we_d):
    n, _, d = ublk.shape
    epd = we_g.shape[0]
    xin = jnp.einsum('srt,std->srd', sel, ublk, preferred_element_type=jnp.float32).astype(jnp.bfloat16)
    xin = xin.reshape(n, epd, CAP, d).transpose(1, 0, 2, 3).reshape(epd, n * CAP, d)
    hg = jnp.einsum('ecd,edf->ecf', xin, we_g, preferred_element_type=jnp.float32)
    hu = jnp.einsum('ecd,edf->ecf', xin, we_u, preferred_element_type=jnp.float32)
    hh = lax.optimization_barrier((jax.nn.silu(hg) * hu).astype(jnp.bfloat16))
    yo = jnp.einsum('ecf,efd->ecd', hh, we_d, preferred_element_type=jnp.float32).astype(jnp.bfloat16)
    return yo.reshape(epd, n, CAP, d)


def weights(g, rank):
    ne, _ = g.shape
    r = jnp.arange(ne * CAP)
    rep = (r[:, None] // CAP == jnp.arange(ne)[None, :]).astype(jnp.bfloat16)
    full = jnp.einsum('et,re->tr', rank, rep, preferred_element_type=jnp.float32)
    sel = (full == (r % CAP).astype(jnp.float32)[None, :])[None]
    w = jnp.einsum('pet,re->ptr', jnp.stack(split3(g)), rep, preferred_element_type=jnp.float32)
    return jnp.where(sel, w, 0.0).astype(jnp.bfloat16)


def solution(mesh):
    ncp = mesh.shape['cp']
    ndev = mesh.shape['b'] * ncp
    tok = P(('dp', 'b'), 'cp', None)
    rep = P()
    exs = P(('b', 'cp'), None, None)

    def layer(x, ids, g_attn, wq, wk, wv, wo, g_ffn, w1, w3, w2, g_moe, wr, we_g, we_u, we_d):
        bd, sd, d = x.shape
        nh = wq.shape[1] // HEAD
        epd = we_g.shape[0]
        nexp = epd * ndev
        nb = ndev // ncp
        ci = lax.axis_index('cp')
        bi = lax.axis_index('b')
        u = rms_norm(x, g_moe).reshape(bd * sd, d)
        uall = lax.all_gather(u, ('b', 'cp'), axis=0, tiled=False)
        info, zero = gates(u, ids, wr, nexp)
        info = lax.all_gather(info, ('b', 'cp'), axis=0, tiled=False)
        pos = ci * sd + jnp.arange(sd)
        n = rms_norm(x, g_attn)
        q = rope(proj(n, wq).reshape(bd, sd, nh, HEAD), pos).reshape(bd, sd, nh, 1, HEAD).transpose(0, 2, 3, 1, 4)
        kv = jnp.stack([rope(proj(n, wk).reshape(bd, sd, nh, HEAD), pos), proj(n, wv).reshape(bd, sd, nh, HEAD)])
        mx = jnp.full((bd, nh, 1, sd), -1e30, jnp.float32)
        den = jnp.zeros((bd, nh, 1, sd), jnp.float32)
        acc = jnp.zeros((bd, nh, 1, sd, HEAD), jnp.float32)
        mx, den, acc = attend(q, kv[0], kv[1], pos, pos, mx, den, acc)
        for step in range(1, ncp):
            kv = lax.ppermute(kv, 'cp', [(j, j + 1) for j in range(step - 1, ncp - 1)])
            kpos = ((ci - step) % ncp) * sd + jnp.arange(sd)
            mx, den, acc = attend(q, kv[0], kv[1], pos, kpos, mx, den, acc)
        o = (acc / den[..., None]).astype(jnp.bfloat16).transpose(0, 3, 1, 2, 4).reshape(bd, sd, nh * HEAD)
        y = (x.astype(jnp.float32) + proj(o, wo).astype(jnp.float32)).astype(jnp.bfloat16)

        g, rank = tables(info, bi * (ncp * epd), ncp * epd)
        g = g.reshape(nb, ncp, ncp * epd, sd)
        rank = rank.reshape(nb, ncp, ncp * epd, sd)
        mine = lax.dynamic_slice_in_dim(rank, ci * epd, epd, axis=2)
        gcol = lax.dynamic_index_in_dim(g, ci, axis=1, keepdims=False)
        rcol = lax.dynamic_index_in_dim(rank, ci, axis=1, keepdims=False)
        peers = [jnp.bitwise_xor(ci, k) for k in range(ncp)]
        order = jnp.asarray(ORDER, jnp.int32)
        blks = [order[bi, i] for i in range(nb)]
        uall = uall.reshape(nb, ncp, sd, d)

        def row_picks(i):
            return pick_rows(lax.dynamic_index_in_dim(mine, blks[i], axis=0, keepdims=False))

        def row_weights(i):
            gi = lax.dynamic_index_in_dim(gcol, blks[i], axis=0, keepdims=False)
            ri = lax.dynamic_index_in_dim(rcol, blks[i], axis=0, keepdims=False)
            gi = jnp.concatenate([lax.dynamic_slice_in_dim(gi, p * epd, epd, axis=0) for p in peers], axis=0)
            ri = jnp.concatenate([lax.dynamic_slice_in_dim(ri, p * epd, epd, axis=0) for p in peers], axis=0)
            return weights(gi, ri).reshape(3 * sd, ncp * epd * CAP)

        def work(ua, i):
            blk = lax.dynamic_index_in_dim(ua, blks[i], axis=0, keepdims=False)
            return expert_rows(blk, sels[i], we_g, we_u, we_d)

        def send(yo):
            got = []
            for k in range(ncp):
                part = lax.dynamic_index_in_dim(yo, peers[k], axis=1, keepdims=False).reshape(epd * CAP, d)
                if k:
                    part = lax.ppermute(part, 'cp', [(j, j ^ k) for j in range(ncp)])
                got.append(part)
            return got

        def total(got, i):
            rows = lax.optimization_barrier(jnp.concatenate(got, axis=0))
            p = lax.optimization_barrier(jnp.dot(ws[i], rows, preferred_element_type=jnp.float32)).reshape(3, sd, d)
            return p[0] + p[1] + p[2]

        tie = lax.optimization_barrier

        def up(v, step):
            return lax.ppermute(v, 'b', [(j, j + 1) for j in range(step)])

        def down(v, step):
            return lax.ppermute(v, 'b', [(nb - 1 - j, nb - 2 - j) for j in range(step)])

        sels = tie([row_picks(i) for i in range(nb)])
        ws = tie([row_weights(i) for i in range(nb)])
        uall, y, sels, ws = tie((uall, y, sels, ws))
        yo1, uall = tie((work(uall, 0), uall))
        g1 = send(yo1)
        yo2, uall, g1[0] = tie((work(uall, 1), uall, g1[0]))
        g2 = send(yo2)
        p1, uall = tie((total(g1, 0), uall))
        up1, dn1 = up(p1, 1), down(p1, 1)
        yo3, uall, g2[0] = tie((work(uall, 2), uall, g2[0]))
        g3 = send(yo3)
        p2, uall = tie((total(g2, 1), uall))
        yo4, g3[0] = tie((work(uall, 3), g3[0]))
        g4 = send(yo4)
        a2, b2 = p2 + up1, p2 + dn1
        p3, a2, b2, y = tie((total(g3, 2), a2, b2, y))
        up2, dn2 = up(a2, 2), down(b2, 2)
        zf = rms_norm(y, g_ffn)
        hh = (jax.nn.silu(jnp.dot(zf, w1, preferred_element_type=jnp.float32)) * jnp.dot(zf, w3, preferred_element_type=jnp.float32)).astype(jnp.bfloat16)
        a3 = jnp.where(bi == 2, p1, p3) + up2
        b3 = jnp.where(bi == 1, p1, p3) + dn2
        hh, a3, b3, g4[0] = tie((hh, a3, b3, g4[0]))
        up3, dn3 = up(a3, 3), down(b3, 3)
        p4 = total(g4, 3)
        f = proj(hh, w2)
        m = (p4 + zero * u.astype(jnp.float32)) + up3 + dn3
        h = y.astype(jnp.float32) + f.astype(jnp.float32) + m.reshape(bd, sd, d)
        return h.astype(jnp.bfloat16)

    return jax.shard_map(layer, mesh=mesh, in_specs=(tok, tok, rep, rep, rep, rep, rep, rep, rep, rep, rep, rep, rep, exs, exs, exs), out_specs=tok, check_vma=False)
```

time: 1490 us -> 1080 us (0.72)
  waiting for transfers between devices: 830 us -> 202 us
  blocking collectives: 0 us -> 140 us
  local copies, waits for them, and re-layouts: 113 us -> 47.6 us
  starting transfers between devices: 9.24 us -> 64.2 us
  matrix products: 429 us -> 467 us
  other arithmetic: 82.9 us -> 120 us
    reduce_scatter x2 -> x0, waiting for transfers between devices: 823 us -> none  [body(): lax.psum_scatter(p, ('b', 'cp'), scatter_dimension=0, tiled=True)]
    ppermute x3 -> x21, waiting for transfers between devices: 5.42 us -> 202 us  [the longest x12 103 us: send(): part = lax.ppermute(part, 'cp', [(j, j ^ k) for j in range(ncp)])]
    all_gather x0 -> x1, blocking collectives: none -> 140 us  [layer(): info = lax.all_gather(info, ('b', 'cp'), axis=0, tiled=False)]
    ppermute x3 -> x21, starting transfers between devices: 9.12 us -> 64.2 us  [the longest x12 33.8 us: send(): part = lax.ppermute(part, 'cp', [(j, j ^ k) for j in range(ncp)])]
    add x3 -> x9, other arithmetic: 0.01 us -> 39.1 us  [the longest x3 17.7 us: total(): return p[0] + p[1] + p[2]]
    broadcast_in_dim x6 -> x12, local copies, waits for them, and re-layouts: 35.4 us -> 0.18 us  [tables(): g = g + jnp.where(hit, info[:, top + j:top + j + 1, :], 0.0)]
    dot_general x10 -> x35, matrix products: 284 us -> 318 us  [the longest x4 56.2 us: expert_rows(): jnp.einsum('ecf,efd->ecd', hh, we_d, preferred_element_type=jnp.float32)]
    transpose x3 -> x4, local copies, waits for them, and re-layouts: 37.7 us -> 6.58 us  [expert_rows(): xin.reshape(n, epd, CAP, d).transpose(1, 0, 2, 3).reshape(epd, n * CAP, d)]
  transfers between devices with their start and end apart: 7 -> 22, of which waited for: 3 -> 7; matrix products, arithmetic and copies ran while one was open for 22% -> 49% of each run, Pallas kernels for 0% -> 0%
where the time goes in v2:
time: 1080 us; the launch traced here: 1060 us
  matrix products  467 us (43%)
  waiting for transfers between devices  202 us (19%)
  blocking collectives  140 us (13%)
  other arithmetic  120 us (11%)
  starting transfers between devices  64.2 us (6%)
  local copies, waits for them, and re-layouts  47.6 us (4%)
  between operations  22.3 us (2%)
    all_gather x1, blocking collectives, layer(): info = lax.all_gather(info, ('b', 'cp'), axis=0, tiled=False)  140 us
    ppermute x12, waiting for transfers between devices, send(): part = lax.ppermute(part, 'cp', [(j, j ^ k) for j in range(ncp)])  103 us
    ppermute x3, waiting for transfers between devices, up(): return lax.ppermute(v, 'b', [(j, j + 1) for j in range(step)])  64.1 us
    dot_general x5, matrix products, proj(): jnp.dot(a, wt, preferred_element_type=jnp.float32).astype(jnp.bfloat16)  61 us
    dot_general x4, matrix products, expert_rows(): jnp.einsum('ecf,efd->ecd', hh, we_d, preferred_element_type=jnp.float32)  56.2 us
    dot_general x4, matrix products, expert_rows(): jnp.einsum('ecd,edf->ecf', xin, we_u, preferred_element_type=jnp.float32)  55.9 us
    dot_general x4, matrix products, attend(): jnp.einsum('bkgqs,bskd->bkgqd', p.astype(jnp.bfloat16), vb, preferred_ele...  51.1 us
    dot_general x4, matrix products, total(): jnp.dot(ws[i], rows, preferred_element_type=jnp.float32)  49.1 us
  transfers between devices with their start and end apart: 22, of which 7 were waited for; matrix products, arithmetic and copies ran while one was open for 49% of the time, Pallas kernels for 0%

profile of v2, /device:TPU:24, one launch (start us, length us, event | category | flops | bytes accessed | tf_op | source)
XLA Modules:
  0.0 1063.0 jit_solution(9997468658104251174)
XLA Ops:
  20.9 10.6 fusion.100
  78.1 139.6 %all-gather = f32[384,512]{1,0:T(8,128)S(1)} all-gather(f32[24,512]{1,0:T(8,128)S(1)} %maximum_bitcast_fusion.1), channel_id=2, replica_groups=mesh['dp'=2,'b'=4,'cp'=4] {'b','cp'}, dimensions={0}, use_global_device_ids=true | all-gather | bytes 835584 | tf_op jit(solution)/shard_map/all_gather | solution.py:136
  343.9 12.2 %fusion.19 = f32[16,512,128]{1,2,0:T(8,128)} fusion(bf16[512,16,128]{0,2,1:T(8,128)(2,1)S(1)} %bitcast.365, f32[16,512,512]{1,2,0:T(8,128)} %get-tuple-element.245, f32[16,512]{1,0:T(8,128)S(1)} %get-tuple-element.225, pred[512,512]{0,1:T(8,128)(4,1)S(1)} %get-tuple-element.234), kind=kOutput, calls=%fused_computation.29 | convolution fusion | flops 1090519040 | bytes 23363584 | tf_op jit(solution)/shard_map/bkgqs,bskd->bkgqd/dot_general | solution.py:44
  356.0 12.5 %fusion.17 = f32[16,512,128]{1,2,0:T(8,128)} fusion(f32[16,512,512]{1,2,0:T(8,128)} %get-tuple-element.243, f32[16,512]{1,0:T(8,128)S(1)} %get-tuple-element.129, pred[512,512]{0,1:T(8,128)(4,1)S(1)} %get-tuple-element.237, bf16[2,1,512,16,128]{4,2,3,1,0:T(8,128)(2,1)} %collective-permute-done), kind=kOutput, calls=%fused_computation.28 | convolution fusion | flops 1090519040 | bytes 23363584 | tf_op jit(solution)/shard_map/bkgqs,bskd->bkgqd/dot_general | solution.py:44
  368.5 12.6 %fusion.15 = f32[16,512,128]{1,2,0:T(8,128)} fusion(f32[16,512,512]{1,2,0:T(8,128)} %get-tuple-element.241, f32[16,512]{1,0:T(8,128)S(1)} %get-tuple-element.128, pred[512,512]{0,1:T(8,128)(4,1)S(1)} %get-tuple-element.236, bf16[2,1,512,16,128]{4,2,3,1,0:T(8,128)(2,1)} %collective-permute-done.1), kind=kOutput, calls=%fused_computation.27 | convolution fusion | flops 1090519040 | bytes 23363584 | tf_op jit(solution)/shard_map/bkgqs,bskd->bkgqd/dot_general | solution.py:44
  381.1 13.9 %divide_convert_fusion = bf16[16,512,128]{1,2,0:T(8,128)(2,1)} fusion(f32[16,512,128]{1,2,0:T(8,128)} %fusion.15, f32[16,512,128]{1,2,0:T(8,128)} %fusion.17, f32[16,512,128]{1,2,0:T(8,128)} %fusion.19, f32[16,512]{1,0:T(8,128)S(1)} %get-tuple-element.123, f32[16,512]{1,0:T(8,128)S(1)} %copy-done.25, f32[16,512]{1,0:T(8,128)S(1)} %copy-done.24, ...), kind=kOutput, calls=%fused_computation.110 | convolution fusion | flops 1099956224 | bytes 34013184 | tf_op jit(solution)/shard_map/bkgqs,bskd->bkgqd/dot_general | solution.py:44
  423.3 12.3 %multiply_convert_fusion.4 = bf16[4,384,1024]{2,1,0:T(8,128)(2,1)} fusion(f32[4,384,1024]{2,1,0:T(8,128)S(1)} %fusion.329, bf16[4,384,2048]{2,1,0:T(8,128)(2,1)S(1)} %bitcast.370, bf16[4,2048,1024]{2,1,0:T(8,128)(2,1)} %param.31), kind=kOutput, calls=%fused_computation.70 | convolution fusion | flops 6451888128 | bytes 32505856 | tf_op jit(solution)/shard_map/ecd,edf->ecf/dot_general | solution.py:102
  435.6 14.9 %convolution_convert_fusion.3 = bf16[4,384,2048]{2,1,0:T(8,128)(2,1)} fusion(bf16[4,384,1024]{2,1,0:T(8,128)(2,1)} %multiply_convert_fusion.4, bf16[4,1024,2048]{2,1,0:T(8,128)(2,1)} %param.32), kind=kOutput, calls=%fused_computation.83 | convolution fusion | flops 6445596672 | bytes 26214400 | tf_op jit(solution)/shard_map/ecf,efd->ecd/dot_general | solution.py:104
  458.5 12.4 %fusion.330 = f32[4,384,1024]{2,1,0:T(8,128)} fusion(bf16[4,384,2048]{2,1,0:T(8,128)(2,1)S(1)} %bitcast.372, bf16[4,2048,1024]{2,1,0:T(8,128)(2,1)} %param.30), kind=kOutput, calls=%fused_computation.495 | convolution fusion | flops 6442450944 | bytes 29360128 | tf_op jit(solution)/shard_map/ecd,edf->ecf/dot_general | solution.py:101
  470.9 15.8 %multiply_convert_fusion.3 = bf16[4,384,1024]{2,1,0:T(8,128)(2,1)} fusion(f32[4,384,1024]{2,1,0:T(8,128)} %fusion.330, bf16[4,384,2048]{2,1,0:T(8,128)(2,1)S(1)} %bitcast.373, bf16[4,2048,1024]{2,1,0:T(8,128)(2,1)} %param.31), kind=kOutput, calls=%fused_computation.69 | convolution fusion | flops 6451888128 | bytes 32505856 | tf_op jit(solution)/shard_map/ecd,edf->ecf/dot_general | solution.py:102
  487.9 24.3 %collective-permute-start.3 = (bf16[384,2048]{1,0:T(8,128)(2,1)S(1)}, bf16[384,2048]{1,0:T(8,128)(2,1)S(1)}, u32[]{:S(2)}, u32[]{:S(2)}) collective-permute-start(bf16[384,2048]{1,0:T(8,128)(2,1)S(1)} %bitcast.393), channel_id=1, source_target_pairs={{0,1},{1,0},{2,3},{3,2},{4,5},{5,4},{6,7},{7,6},{8,9},{9,8},{10,11... | collective-permute-start | bytes 4718600 | tf_op jit(solution)/shard_map/ppermute | solution.py:182
  515.3 13.2 %convolution_convert_fusion.2 = bf16[4,384,2048]{2,1,0:T(8,128)(2,1)S(1)} fusion(bf16[4,384,1024]{2,1,0:T(8,128)(2,1)} %multiply_convert_fusion.3, bf16[4,1024,2048]{2,1,0:T(8,128)(2,1)} %param.32), kind=kOutput, calls=%fused_computation.82 | convolution fusion | flops 6445596672 | bytes 26214400 | tf_op jit(solution)/shard_map/ecf,efd->ecd/dot_general | solution.py:104
  532.9 17.6 %collective-permute-done.4 = bf16[384,2048]{1,0:T(8,128)(2,1)S(1)} collective-permute-done((bf16[384,2048]{1,0:T(8,128)(2,1)S(1)}, bf16[384,2048]{1,0:T(8,128)(2,1)S(1)}, u32[]{:S(2)}, u32[]{:S(2)}) %collective-permute-start.4) | collective-permute-done | bytes 1572896 | tf_op jit(solution)/shard_map/ppermute | solution.py:182
  550.5 33.2 %collective-permute-done.5 = bf16[384,2048]{1,0:T(8,128)(2,1)S(1)} collective-permute-done((bf16[384,2048]{1,0:T(8,128)(2,1)S(1)}, bf16[384,2048]{1,0:T(8,128)(2,1)S(1)}, u32[]{:S(2)}, u32[]{:S(2)}) %collective-permute-start.5) | collective-permute-done | bytes 1572896 | tf_op jit(solution)/shard_map/ppermute | solution.py:182
  584.8 12.1 %fusion.331 = f32[1536,2048]{1,0:T(8,128)S(1)} fusion(bf16[1536,1536]{1,0:T(8,128)(2,1)} %bitcast.415, bf16[1536,2048]{1,0:T(8,128)(2,1)S(1)} %pad_maximum_fusion), kind=kOutput, calls=%fused_computation.496 | convolution fusion | flops 9663676416 | bytes 23592960 | tf_op jit(solution)/shard_map/dot_general | solution.py:188
  614.2 10.4 fusion.332
  624.6 12.0 %multiply_convert_fusion.2 = bf16[4,384,1024]{2,1,0:T(8,128)(2,1)} fusion(f32[4,384,1024]{2,1,0:T(8,128)S(1)} %fusion.332, bf16[4,384,2048]{2,1,0:T(8,128)(2,1)S(1)} %bitcast.376, bf16[4,2048,1024]{2,1,0:T(8,128)(2,1)} %param.31), kind=kOutput, calls=%fused_computation.68 | convolution fusion | flops 6451888128 | bytes 32505856 | tf_op jit(solution)/shard_map/ecd,edf->ecf/dot_general | solution.py:102
  636.6 14.8 %convolution_convert_fusion.1 = bf16[4,384,2048]{2,1,0:T(8,128)(2,1)} fusion(bf16[4,384,1024]{2,1,0:T(8,128)(2,1)} %multiply_convert_fusion.2, bf16[4,1024,2048]{2,1,0:T(8,128)(2,1)} %param.32), kind=kOutput, calls=%fused_computation.81 | convolution fusion | flops 6445596672 | bytes 26214400 | tf_op jit(solution)/shard_map/ecf,efd->ecd/dot_general | solution.py:104
  655.4 12.6 %fusion.333 = f32[1536,2048]{1,0:T(8,128)} fusion(bf16[1536,1536]{1,0:T(8,128)(2,1)S(1)} %bitcast.414, bf16[1536,2048]{1,0:T(8,128)(2,1)S(1)} %pad_maximum_fusion.1), kind=kOutput, calls=%fused_computation.498 | convolution fusion | flops 9663676416 | bytes 23592960 | tf_op jit(solution)/shard_map/dot_general | solution.py:188
  684.2 15.4 %fusion.334 = f32[4,384,1024]{2,1,0:T(8,128)} fusion(bf16[4,384,2048]{2,1,0:T(8,128)(2,1)} %bitcast.377, bf16[4,2048,1024]{2,1,0:T(8,128)(2,1)} %param.30), kind=kOutput, calls=%fused_computation.499 | convolution fusion | flops 6442450944 | bytes 29360128 | tf_op jit(solution)/shard_map/ecd,edf->ecf/dot_general | solution.py:101
  699.6 15.8 %multiply_convert_fusion.1 = bf16[4,384,1024]{2,1,0:T(8,128)(2,1)} fusion(f32[4,384,1024]{2,1,0:T(8,128)} %fusion.334, bf16[4,384,2048]{2,1,0:T(8,128)(2,1)S(1)} %bitcast.378, bf16[4,2048,1024]{2,1,0:T(8,128)(2,1)} %param.31), kind=kOutput, calls=%fused_computation.67 | convolution fusion | flops 6451888128 | bytes 32505856 | tf_op jit(solution)/shard_map/ecd,edf->ecf/dot_general | solution.py:102
  722.9 13.3 %convolution_convert_fusion = bf16[4,384,2048]{2,1,0:T(8,128)(2,1)S(1)} fusion(bf16[4,384,1024]{2,1,0:T(8,128)(2,1)} %multiply_convert_fusion.1, bf16[4,1024,2048]{2,1,0:T(8,128)(2,1)} %param.32), kind=kOutput, calls=%fused_computation.80 | convolution fusion | flops 6445596672 | bytes 26214400 | tf_op jit(solution)/shard_map/ecf,efd->ecd/dot_general | solution.py:104
  738.5 19.5 %collective-permute-done.10 = bf16[384,2048]{1,0:T(8,128)(2,1)S(1)} collective-permute-done((bf16[384,2048]{1,0:T(8,128)(2,1)S(1)}, bf16[384,2048]{1,0:T(8,128)(2,1)S(1)}, u32[]{:S(2)}, u32[]{:S(2)}) %collective-permute-start.10) | collective-permute-done | bytes 1572896 | tf_op jit(solution)/shard_map/ppermute | solution.py:182
  758.0 32.9 %collective-permute-done.11 = bf16[384,2048]{1,0:T(8,128)(2,1)S(1)} collective-permute-done((bf16[384,2048]{1,0:T(8,128)(2,1)}, bf16[384,2048]{1,0:T(8,128)(2,1)S(1)}, u32[]{:S(2)}, u32[]{:S(2)}) %collective-permute-start.11) | collective-permute-done | bytes 1572896 | tf_op jit(solution)/shard_map/ppermute | solution.py:182
  796.1 12.2 %fusion.335 = f32[1536,2048]{1,0:T(8,128)} fusion(bf16[1536,1536]{1,0:T(8,128)(2,1)S(1)} %bitcast.411, bf16[1536,2048]{1,0:T(8,128)(2,1)S(1)} %pad_maximum_fusion.2), kind=kOutput, calls=%fused_computation.500 | convolution fusion | flops 9663676416 | bytes 23592960 | tf_op jit(solution)/shard_map/dot_general | solution.py:188
  831.7 27.6 %fusion.113 = f32[512,8192]{1,0:T(8,128)} fusion(bf16[2048,8192]{1,0:T(8,128)(2,1)} %param.25, bf16[1,512,2048]{2,1,0:T(8,128)(2,1)} %fusion.68, f32[2048]{0:T(1024)S(1)} %copy-done.26, f32[512]{0:T(512)S(1)} %add_rsqrt_fusion), kind=kOutput, calls=%fused_computation.166 | convolution fusion | flops 17184063488 | bytes 52439040 | tf_op jit(solution)/shard_map/dot_general | solution.py:217
  859.3 27.1 %fusion.12 = bf16[1,512,8192]{2,1,0:T(8,128)(2,1)} fusion(bf16[2048,8192]{1,0:T(8,128)(2,1)} %param.26, f32[512,8192]{1,0:T(8,128)} %fusion.113, bf16[1,512,2048]{2,1,0:T(8,128)(2,1)} %fusion.68, f32[2048]{0:T(1024)S(1)} %copy-done.26, f32[512]{0:T(512)S(1)} %add_rsqrt_fusion), kind=kOutput, calls=%fused_computation.21 | convolution fusion | flops 17209229312 | bytes 60827648 | tf_op jit(solution)/shard_map/dot_general | solution.py:217
  886.5 33.3 %collective-permute-done.15 = f32[512,2048]{1,0:T(8,128)} collective-permute-done((f32[512,2048]{1,0:T(8,128)}, f32[512,2048]{1,0:T(8,128)}, u32[]{:S(2)}, u32[]{:S(2)}) %collective-permute-start.15) | collective-permute-done | bytes 4194336 | tf_op jit(solution)/shard_map/ppermute | solution.py:197
  919.8 11.9 %select_add_fusion = (f32[512,2048]{1,0:T(8,128)}, f32[512,2048]{1,0:T(8,128)}) fusion(f32[512,2048]{1,0:T(8,128)} %collective-permute-done.15, f32[512,2048]{1,0:T(8,128)} %slice_add_fusion.6, f32[512,2048]{1,0:T(8,128)} %slice_add_fusion.2, pred[]{:T(512)S(6)} %eq.567, f32[512,2048]{1,0:T(8,128)} %collective-permute-done.14, pred[]{:T(512)S(6)} %eq.566), kind=kLoop, calls=%fused_computation.108 | loop fusion | flops 4194304 | bytes 25165826 | tf_op jit(solution)/shard_map/add | solution.py:219
  950.3 12.2 %fusion.336 = f32[1536,2048]{1,0:T(8,128)} fusion(bf16[1536,1536]{1,0:T(8,128)(2,1)S(1)} %bitcast.408, bf16[1536,2048]{1,0:T(8,128)(2,1)S(1)} %pad_maximum_fusion.3), kind=kOutput, calls=%fused_computation.501 | convolution fusion | flops 9663676416 | bytes 23592960 | tf_op jit(solution)/shard_map/dot_general | solution.py:188
  962.6 64.1 %collective-permute-done.19 = f32[512,2048]{1,0:T(8,128)S(1)} collective-permute-done((f32[512,2048]{1,0:T(8,128)}, f32[512,2048]{1,0:T(8,128)S(1)}, u32[]{:S(2)}, u32[]{:S(2)}) %collective-permute-start.19) | collective-permute-done | bytes 4194336 | tf_op jit(solution)/shard_map/ppermute | solution.py:194
  1028.2 27.5 %fusion.73 = bf16[1,512,2048]{2,1,0:T(8,128)(2,1)} fusion(bf16[1,512,2048]{2,1,0:T(8,128)(2,1)S(1)} %copy-done.18, f32[512,2048]{1,0:T(8,128)} %collective-permute-done.20, f32[512,2048]{1,0:T(8,128)S(1)} %collective-permute-done.19, f32[1536,2048]{1,0:T(8,128)} %fusion.336, bf16[1,512,2048]{2,1,0:T(8,128)(2,1)S(1)} %copy-done.8, f32[512]{0:T(512)S(1)} %copy-done.29, ...), kind=kOutput, calls=%fused_computation.92 | convolution fusion | flops 17193500672 | bytes 69208064 | tf_op jit(solution)/shard_map/dot_general | solution.py:34
  (249 shorter events, 320.6 us)
Async XLA Ops:
  6.5 68.1 %copy-start = (bf16[2048,96]{0,1:T(8,128)(2,1)S(1)}, bf16[2048,96]{0,1:T(8,128)(2,1)}, u32[]{:S(2)}) copy-start(bf16[2048,96]{0,1:T(8,128)(2,1)} %param.29) | copy-start | bytes 1179652
  6.5 398.5 %all-gather.3.cloned.1.call-start = ((), (), s32[]{:S(2)}) async-start(), calls=%async_computation | async-start | bytes 35651584 | tf_op jit(solution)/shard_map/all_gather | solution.py:134
  20.0 16.1 %slice-start.2 = ((s8[8388608]{0:T(1024)(128)(4,1)}), s8[4194304]{0:T(1024)(128)(4,1)S(1)}, s32[]{:S(2)}) async-start(s8[8388608]{0:T(1024)(128)(4,1)} %bitcast.404), calls=%async_computation.3 | async-start | bytes 8388608
  62.8 165.4 %collective-permute-start = (bf16[2,1,512,16,128]{4,2,3,1,0:T(8,128)(2,1)}, bf16[2,1,512,16,128]{4,2,3,1,0:T(8,128)(2,1)}, u32[]{:S(2)}, u32[]{:S(2)}) collective-permute-start(bf16[2,1,512,16,128]{4,2,3,1,0:T(8,128)(2,1)} %pad_maximum_fusion.4), channel_id=1, source_target_pairs={{0,1},{1,2},{2,3},{4,5},{5,6},{6,7},{8,9},{9,10},{10,11},{12,13},{... | collective-permute-start | bytes 12582920 | tf_op jit(solution)/shard_map/ppermute | solution.py:146
  228.2 26.3 %collective-permute-start.1 = (bf16[2,1,512,16,128]{4,2,3,1,0:T(8,128)(2,1)}, bf16[2,1,512,16,128]{4,2,3,1,0:T(8,128)(2,1)}, u32[]{:S(2)}, u32[]{:S(2)}) collective-permute-start(bf16[2,1,512,16,128]{4,2,3,1,0:T(8,128)(2,1)} %collective-permute-done), channel_id=1, source_target_pairs={{1,2},{2,3},{5,6},{6,7},{9,10},{10,11},{13,14},{14,15},{17,18},{18... | collective-permute-start | bytes 12582920 | tf_op jit(solution)/shard_map/ppermute | solution.py:146
  254.4 42.3 %collective-permute-start.2 = (bf16[2,1,512,16,128]{4,2,3,1,0:T(8,128)(2,1)}, bf16[2,1,512,16,128]{4,2,3,1,0:T(8,128)(2,1)}, u32[]{:S(2)}, u32[]{:S(2)}) collective-permute-start(bf16[2,1,512,16,128]{4,2,3,1,0:T(8,128)(2,1)} %collective-permute-done.1), channel_id=1, source_target_pairs={{2,3},{6,7},{10,11},{14,15},{18,19},{22,23},{26,27},{30,31}} | collective-permute-start | bytes 12582920 | tf_op jit(solution)/shard_map/ppermute | solution.py:146
  458.4 28.3 %slice-start = ((s8[6291456]{0:T(1024)(128)(4,1)}), s8[4194304]{0:T(1024)(128)(4,1)S(1)}, s32[]{:S(2)}) async-start(s8[6291456]{0:T(1024)(128)(4,1)} %bitcast.380), calls=%async_computation.1 | async-start | bytes 8388608
  470.9 15.8 %slice-start.1 = ((s8[6291456]{0:T(1024)(128)(4,1)}), s8[2097152]{0:T(1024)(128)(4,1)S(1)}, s32[]{:S(2)}) async-start(s8[6291456]{0:T(1024)(128)(4,1)} %bitcast.380), calls=%async_computation.2 | async-start | bytes 4194304
  487.9 45.0 %collective-permute-start.3 = (bf16[384,2048]{1,0:T(8,128)(2,1)S(1)}, bf16[384,2048]{1,0:T(8,128)(2,1)S(1)}, u32[]{:S(2)}, u32[]{:S(2)}) collective-permute-start(bf16[384,2048]{1,0:T(8,128)(2,1)S(1)} %bitcast.393), channel_id=1, source_target_pairs={{0,1},{1,0},{2,3},{3,2},{4,5},{5,4},{6,7},{7,6},{8,9},{9,8},{10,11... | collective-permute-start | bytes 4718600 | tf_op jit(solution)/shard_map/ppermute | solution.py:182
  512.2 38.3 %collective-permute-start.4 = (bf16[384,2048]{1,0:T(8,128)(2,1)S(1)}, bf16[384,2048]{1,0:T(8,128)(2,1)S(1)}, u32[]{:S(2)}, u32[]{:S(2)}) collective-permute-start(bf16[384,2048]{1,0:T(8,128)(2,1)S(1)} %bitcast.392), channel_id=1, source_target_pairs={{0,2},{1,3},{2,0},{3,1},{4,6},{5,7},{6,4},{7,5},{8,10},{9,11},{10,... | collective-permute-start | bytes 4718600 | tf_op jit(solution)/shard_map/ppermute | solution.py:182
  515.3 68.5 %collective-permute-start.5 = (bf16[384,2048]{1,0:T(8,128)(2,1)S(1)}, bf16[384,2048]{1,0:T(8,128)(2,1)S(1)}, u32[]{:S(2)}, u32[]{:S(2)}) collective-permute-start(bf16[384,2048]{1,0:T(8,128)(2,1)S(1)} %bitcast.391), channel_id=1, source_target_pairs={{0,3},{1,2},{2,1},{3,0},{4,7},{5,6},{6,5},{7,4},{8,11},{9,10},{10,... | collective-permute-start | bytes 4718600 | tf_op jit(solution)/shard_map/ppermute | solution.py:182
  530.8 120.6 %collective-permute-start.6 = (bf16[384,2048]{1,0:T(8,128)(2,1)}, bf16[384,2048]{1,0:T(8,128)(2,1)}, u32[]{:S(2)}, u32[]{:S(2)}) collective-permute-start(bf16[384,2048]{1,0:T(8,128)(2,1)} %bitcast.113), channel_id=1, source_target_pairs={{0,1},{1,0},{2,3},{3,2},{4,5},{5,4},{6,7},{7,6},{8,9},{9,8},{10,11... | collective-permute-start | bytes 4718600 | tf_op jit(solution)/shard_map/ppermute | solution.py:182
  531.0 120.5 %collective-permute-start.7 = (bf16[384,2048]{1,0:T(8,128)(2,1)}, bf16[384,2048]{1,0:T(8,128)(2,1)}, u32[]{:S(2)}, u32[]{:S(2)}) collective-permute-start(bf16[384,2048]{1,0:T(8,128)(2,1)} %bitcast.114), channel_id=1, source_target_pairs={{0,2},{1,3},{2,0},{3,1},{4,6},{5,7},{6,4},{7,5},{8,10},{9,11},{10,... | collective-permute-start | bytes 4718600 | tf_op jit(solution)/shard_map/ppermute | solution.py:182
  532.9 118.6 %collective-permute-start.8 = (bf16[384,2048]{1,0:T(8,128)(2,1)}, bf16[384,2048]{1,0:T(8,128)(2,1)}, u32[]{:S(2)}, u32[]{:S(2)}) collective-permute-start(bf16[384,2048]{1,0:T(8,128)(2,1)} %bitcast.115), channel_id=1, source_target_pairs={{0,3},{1,2},{2,1},{3,0},{4,7},{5,6},{6,5},{7,4},{8,11},{9,10},{10,... | collective-permute-start | bytes 4718600 | tf_op jit(solution)/shard_map/ppermute | solution.py:182
  600.2 216.6 %collective-permute-start.12 = (f32[512,2048]{1,0:T(8,128)}, f32[512,2048]{1,0:T(8,128)}, u32[]{:S(2)}, u32[]{:S(2)}) collective-permute-start(f32[512,2048]{1,0:T(8,128)} %slice_add_fusion.6), channel_id=1, source_target_pairs={{0,4},{1,5},{2,6},{3,7},{16,20},{17,21},{18,22},{19,23}} | collective-permute-start | bytes 12582920 | tf_op jit(solution)/shard_map/ppermute | solution.py:194
  602.9 213.8 %collective-permute-start.13 = (f32[512,2048]{1,0:T(8,128)}, f32[512,2048]{1,0:T(8,128)}, u32[]{:S(2)}, u32[]{:S(2)}) collective-permute-start(f32[512,2048]{1,0:T(8,128)} %slice_add_fusion.6), channel_id=1, source_target_pairs={{12,8},{13,9},{14,10},{15,11},{28,24},{29,25},{30,26},{31,27}} | collective-permute-start | bytes 12582920 | tf_op jit(solution)/shard_map/ppermute | solution.py:197
  720.7 37.3 %collective-permute-start.10 = (bf16[384,2048]{1,0:T(8,128)(2,1)S(1)}, bf16[384,2048]{1,0:T(8,128)(2,1)S(1)}, u32[]{:S(2)}, u32[]{:S(2)}) collective-permute-start(bf16[384,2048]{1,0:T(8,128)(2,1)S(1)} %bitcast.394), channel_id=1, source_target_pairs={{0,2},{1,3},{2,0},{3,1},{4,6},{5,7},{6,4},{7,5},{8,10},{9,11},{10,... | collective-permute-start | bytes 4718600 | tf_op jit(solution)/shard_map/ppermute | solution.py:182
  722.1 68.7 %collective-permute-start.11 = (bf16[384,2048]{1,0:T(8,128)(2,1)}, bf16[384,2048]{1,0:T(8,128)(2,1)S(1)}, u32[]{:S(2)}, u32[]{:S(2)}) collective-permute-start(bf16[384,2048]{1,0:T(8,128)(2,1)} %bitcast.124), channel_id=1, source_target_pairs={{0,3},{1,2},{2,1},{3,0},{4,7},{5,6},{6,5},{7,4},{8,11},{9,10},{10,... | collective-permute-start | bytes 4718600 | tf_op jit(solution)/shard_map/ppermute | solution.py:182
  722.7 70.3 %collective-permute-start.9 = (bf16[384,2048]{1,0:T(8,128)(2,1)}, bf16[384,2048]{1,0:T(8,128)(2,1)}, u32[]{:S(2)}, u32[]{:S(2)}) collective-permute-start(bf16[384,2048]{1,0:T(8,128)(2,1)} %bitcast.122), channel_id=1, source_target_pairs={{0,1},{1,0},{2,3},{3,2},{4,5},{5,4},{6,7},{7,6},{8,9},{9,8},{10,11... | collective-permute-start | bytes 4718600 | tf_op jit(solution)/shard_map/ppermute | solution.py:182
  758.0 182.5 %collective-permute-start.16 = (bf16[384,2048]{1,0:T(8,128)(2,1)}, bf16[384,2048]{1,0:T(8,128)(2,1)S(1)}, u32[]{:S(2)}, u32[]{:S(2)}) collective-permute-start(bf16[384,2048]{1,0:T(8,128)(2,1)} %bitcast.130), channel_id=1, source_target_pairs={{0,1},{1,0},{2,3},{3,2},{4,5},{5,4},{6,7},{7,6},{8,9},{9,8},{10,11... | collective-permute-start | bytes 4718600 | tf_op jit(solution)/shard_map/ppermute | solution.py:182
  790.9 149.6 %collective-permute-start.17 = (bf16[384,2048]{1,0:T(8,128)(2,1)}, bf16[384,2048]{1,0:T(8,128)(2,1)}, u32[]{:S(2)}, u32[]{:S(2)}) collective-permute-start(bf16[384,2048]{1,0:T(8,128)(2,1)} %bitcast.131), channel_id=1, source_target_pairs={{0,2},{1,3},{2,0},{3,1},{4,6},{5,7},{6,4},{7,5},{8,10},{9,11},{10,... | collective-permute-start | bytes 4718600 | tf_op jit(solution)/shard_map/ppermute | solution.py:182
  793.0 147.5 %collective-permute-start.18 = (bf16[384,2048]{1,0:T(8,128)(2,1)}, bf16[384,2048]{1,0:T(8,128)(2,1)}, u32[]{:S(2)}, u32[]{:S(2)}) collective-permute-start(bf16[384,2048]{1,0:T(8,128)(2,1)} %bitcast.132), channel_id=1, source_target_pairs={{0,3},{1,2},{2,1},{3,0},{4,7},{5,6},{6,5},{7,4},{8,11},{9,10},{10,... | collective-permute-start | bytes 4718600 | tf_op jit(solution)/shard_map/ppermute | solution.py:182
  825.3 61.2 %collective-permute-start.14 = (f32[512,2048]{1,0:T(8,128)}, f32[512,2048]{1,0:T(8,128)}, u32[]{:S(2)}, u32[]{:S(2)}) collective-permute-start(f32[512,2048]{1,0:T(8,128)} %get-tuple-element.77), channel_id=1, source_target_pairs={{0,4},{4,8},{1,5},{5,9},{2,6},{6,10},{3,7},{7,11},{16,20},{20,24},... | collective-permute-start | bytes 12582920 | tf_op jit(solution)/shard_map/ppermute | solution.py:194
  828.0 91.8 %collective-permute-start.15 = (f32[512,2048]{1,0:T(8,128)}, f32[512,2048]{1,0:T(8,128)}, u32[]{:S(2)}, u32[]{:S(2)}) collective-permute-start(f32[512,2048]{1,0:T(8,128)} %get-tuple-element.78), channel_id=1, source_target_pairs={{12,8},{8,4},{13,9},{9,5},{14,10},{10,6},{15,11},{11,7},{28,24},{2... | collective-permute-start | bytes 12582920 | tf_op jit(solution)/shard_map/ppermute | solution.py:197
  931.7 18.5 %slice-start.4 = ((s8[4718592]{0:T(1024)(128)(4,1)}), s8[4194304]{0:T(1024)(128)(4,1)S(1)}, s32[]{:S(2)}) async-start(s8[4718592]{0:T(1024)(128)(4,1)} %bitcast.406), calls=%async_computation.5 | async-start | bytes 8388608
  931.7 18.6 %slice-start.5 = ((s8[4718592]{0:T(1024)(128)(4,1)}), s8[524288]{0:T(1024)(128)(4,1)S(1)}, s32[]{:S(2)}) async-start(s8[4718592]{0:T(1024)(128)(4,1)} %bitcast.406), calls=%async_computation.6 | async-start | bytes 1048576
  931.7 95.0 %collective-permute-start.19 = (f32[512,2048]{1,0:T(8,128)}, f32[512,2048]{1,0:T(8,128)S(1)}, u32[]{:S(2)}, u32[]{:S(2)}) collective-permute-start(f32[512,2048]{1,0:T(8,128)} %get-tuple-element.83), channel_id=1, source_target_pairs={{0,4},{4,8},{8,12},{1,5},{5,9},{9,13},{2,6},{6,10},{10,14},{3,7},{... | collective-permute-start | bytes 12582920 | tf_op jit(solution)/shard_map/ppermute | solution.py:194
  933.3 94.9 %collective-permute-start.20 = (f32[512,2048]{1,0:T(8,128)}, f32[512,2048]{1,0:T(8,128)}, u32[]{:S(2)}, u32[]{:S(2)}) collective-permute-start(f32[512,2048]{1,0:T(8,128)} %get-tuple-element.84), channel_id=1, source_target_pairs={{12,8},{8,4},{4,0},{13,9},{9,5},{5,1},{14,10},{10,6},{6,2},{15,11}... | collective-permute-start | bytes 12582920 | tf_op jit(solution)/shard_map/ppermute | solution.py:197
  950.3 77.9 %copy-start.8 = (bf16[1,512,2048]{2,1,0:T(8,128)(2,1)S(1)}, bf16[1,512,2048]{2,1,0:T(8,128)(2,1)}, u32[]{:S(2)}) copy-start(bf16[1,512,2048]{2,1,0:T(8,128)(2,1)} %fusion.65) | copy-start | bytes 6291460
  950.3 77.9 %copy-start.18 = (bf16[1,512,2048]{2,1,0:T(8,128)(2,1)S(1)}, bf16[1,512,2048]{2,1,0:T(8,128)(2,1)}, u32[]{:S(2)}) copy-start(bf16[1,512,2048]{2,1,0:T(8,128)(2,1)} %fusion.68) | copy-start | bytes 6291460
  950.3 77.9 %copy-start.29 = (f32[512]{0:T(512)S(1)}, f32[512]{0:T(512)}, u32[]{:S(2)}) copy-start(f32[512]{0:T(512)} %get-tuple-element.97) | copy-start | bytes 6148
  1028.2 27.5 %copy-start.1 = (bf16[2048,96]{0,1:T(8,128)(2,1)S(1)}, bf16[2048,96]{0,1:T(8,128)(2,1)}, u32[]{:S(2)}) copy-start(bf16[2048,96]{0,1:T(8,128)(2,1)} %param.29) | copy-start | bytes 1179652
  (31 other events, 259.4 us)
Sparse Core Ops, SparseCore 0:
  13.1 217.2 all-gather.2

commit v3 on v2

--- a/solution.py
+++ b/solution.py
@@ -131,11 +131,12 @@
         ci = lax.axis_index('cp')
         bi = lax.axis_index('b')
         u = rms_norm(x, g_moe).reshape(bd * sd, d)
-        uall = lax.all_gather(u, ('b', 'cp'), axis=0, tiled=False)
         info, zero = gates(u, ids, wr, nexp)
         info = lax.all_gather(info, ('b', 'cp'), axis=0, tiled=False)
+        info, usend, xa = lax.optimization_barrier((info, u, x))
+        uall = lax.all_gather(usend, ('b', 'cp'), axis=0, tiled=False)
         pos = ci * sd + jnp.arange(sd)
-        n = rms_norm(x, g_attn)
+        n = rms_norm(xa, g_attn)
         q = rope(proj(n, wq).reshape(bd, sd, nh, HEAD), pos).reshape(bd, sd, nh, 1, HEAD).transpose(0, 2, 3, 1, 4)
         kv = jnp.stack([rope(proj(n, wk).reshape(bd, sd, nh, HEAD), pos), proj(n, wv).reshape(bd, sd, nh, HEAD)])
         mx = jnp.full((bd, nh, 1, sd), -1e30, jnp.float32)
@@ -196,8 +197,8 @@
         def down(v, step):
             return lax.ppermute(v, 'b', [(nb - 1 - j, nb - 2 - j) for j in range(step)])
 
+        ws = tie([row_weights(i) for i in range(nb)])
         sels = tie([row_picks(i) for i in range(nb)])
-        ws = tie([row_weights(i) for i in range(nb)])
         uall, y, sels, ws = tie((uall, y, sels, ws))
         yo1, uall = tie((work(uall, 0), uall))
         g1 = send(yo1)
@@ -208,11 +209,11 @@
         yo3, uall, g2[0] = tie((work(uall, 2), uall, g2[0]))
         g3 = send(yo3)
         p2, uall = tie((total(g2, 1), uall))
-        yo4, g3[0] = tie((work(uall, 3), g3[0]))
+        yo4, g3[0], p2 = tie((work(uall, 3), g3[0], p2))
         g4 = send(yo4)
-        a2, b2 = p2 + up1, p2 + dn1
-        p3, a2, b2, y = tie((total(g3, 2), a2, b2, y))
+        a2, b2, g3[0] = tie((p2 + up1, p2 + dn1, g3[0]))
         up2, dn2 = up(a2, 2), down(b2, 2)
+        p3, y = tie((total(g3, 2), y))
         zf = rms_norm(y, g_ffn)
         hh = (jax.nn.silu(jnp.dot(zf, w1, preferred_element_type=jnp.float32)) * jnp.dot(zf, w3, preferred_element_type=jnp.float32)).astype(jnp.bfloat16)
         a3 = jnp.where(bi == 2, p1, p3) + up2
@@ -220,7 +221,7 @@
         hh, a3, b3, g4[0] = tie((hh, a3, b3, g4[0]))
         up3, dn3 = up(a3, 3), down(b3, 3)
         p4 = total(g4, 3)
-        f = proj(hh, w2)
+        f = lax.optimization_barrier(proj(hh, w2))
         m = (p4 + zero * u.astype(jnp.float32)) + up3 + dn3
         h = y.astype(jnp.float32) + f.astype(jnp.float32) + m.reshape(bd, sd, d)
         return h.astype(jnp.bfloat16)

time: 1080 us -> 1100 us (1.019)
  starting transfers between devices: 64.2 us -> 206 us
  blocking collectives: 140 us -> 19 us
  waiting for transfers between devices: 202 us -> 182 us
    ppermute x12, starting transfers between devices: 33.8 us -> 176 us  [send(): part = lax.ppermute(part, 'cp', [(j, j ^ k) for j in range(ncp)])]
    all_gather x1, blocking collectives: 140 us -> 19 us  [layer(): info = lax.all_gather(info, ('b', 'cp'), axis=0, tiled=False)]
    ppermute x12, waiting for transfers between devices: 103 us -> 89.3 us  [send(): part = lax.ppermute(part, 'cp', [(j, j ^ k) for j in range(ncp)])]
where the time goes in v3:
time: 1100 us; the launch traced here: 1080 us
  matrix products  477 us (43%)
  starting transfers between devices  206 us (19%)
  waiting for transfers between devices  182 us (17%)
  other arithmetic  125 us (11%)
  local copies, waits for them, and re-layouts  52.1 us (5%)
  between operations  22 us (2%)
  blocking collectives  19 us (2%)
    ppermute x12, starting transfers between devices, send(): part = lax.ppermute(part, 'cp', [(j, j ^ k) for j in range(ncp)])  176 us
    ppermute x12, waiting for transfers between devices, send(): part = lax.ppermute(part, 'cp', [(j, j ^ k) for j in range(ncp)])  89.3 us
    ppermute x3, waiting for transfers between devices, up(): return lax.ppermute(v, 'b', [(j, j + 1) for j in range(step)])  62.2 us
    dot_general x4, matrix products, expert_rows(): jnp.einsum('ecd,edf->ecf', xin, we_u, preferred_element_type=jnp.float32)  60.2 us
    dot_general x4, matrix products, expert_rows(): jnp.einsum('ecf,efd->ecd', hh, we_d, preferred_element_type=jnp.float32)  57.6 us
    dot_general x4, matrix products, expert_rows(): jnp.einsum('ecd,edf->ecf', xin, we_g, preferred_element_type=jnp.float32)  53.3 us
    dot_general x5, matrix products, proj(): jnp.dot(a, wt, preferred_element_type=jnp.float32).astype(jnp.bfloat16)  51.6 us
    dot_general x4, matrix products, attend(): jnp.einsum('bkgqs,bskd->bkgqd', p.astype(jnp.bfloat16), vb, preferred_ele...  50.8 us
  transfers between devices with their start and end apart: 22, of which 7 were waited for; matrix products, arithmetic and copies ran while one was open for 49% of the time, Pallas kernels for 0%

profile of v3, /device:TPU:24, one launch (start us, length us, event | category | flops | bytes accessed | tf_op | source)
XLA Modules:
  0.0 1083.8 jit_solution(2677411221306355759)
XLA Ops:
  17.1 19.0 %all-gather = f32[384,512]{1,0:T(8,128)S(1)} all-gather(f32[24,512]{1,0:T(8,128)S(1)} %maximum_bitcast_fusion.1), channel_id=2, replica_groups=mesh['dp'=2,'b'=4,'cp'=4] {'b','cp'}, dimensions={0}, use_global_device_ids=true | all-gather | bytes 835584 | tf_op jit(solution)/shard_map/all_gather | solution.py:135
  214.9 12.9 %fusion.19 = f32[16,512,128]{1,2,0:T(8,128)} fusion(bf16[512,16,128]{0,2,1:T(8,128)(2,1)} %bitcast.375, f32[16,512,512]{1,2,0:T(8,128)} %get-tuple-element.233, f32[16,512]{1,0:T(8,128)S(1)} %get-tuple-element.213, pred[512,512]{0,1:T(8,128)(4,1)S(1)} %get-tuple-element.222), kind=kOutput, calls=%fused_computation.29 | convolution fusion | flops 1090519040 | bytes 23363584 | tf_op jit(solution)/shard_map/bkgqs,bskd->bkgqd/dot_general | solution.py:44
  227.8 12.5 %fusion.17 = f32[16,512,128]{1,2,0:T(8,128)} fusion(f32[16,512,512]{1,2,0:T(8,128)} %get-tuple-element.231, f32[16,512]{1,0:T(8,128)S(1)} %get-tuple-element.115, pred[512,512]{0,1:T(8,128)(4,1)S(1)} %get-tuple-element.225, bf16[2,1,512,16,128]{4,2,3,1,0:T(8,128)(2,1)} %collective-permute-done), kind=kOutput, calls=%fused_computation.28 | convolution fusion | flops 1090519040 | bytes 23363584 | tf_op jit(solution)/shard_map/bkgqs,bskd->bkgqd/dot_general | solution.py:44
  240.3 12.6 %fusion.15 = f32[16,512,128]{1,2,0:T(8,128)} fusion(f32[16,512,512]{1,2,0:T(8,128)} %get-tuple-element.229, f32[16,512]{1,0:T(8,128)S(1)} %get-tuple-element.114, pred[512,512]{0,1:T(8,128)(4,1)S(1)} %get-tuple-element.224, bf16[2,1,512,16,128]{4,2,3,1,0:T(8,128)(2,1)} %collective-permute-done.1), kind=kOutput, calls=%fused_computation.27 | convolution fusion | flops 1090519040 | bytes 23363584 | tf_op jit(solution)/shard_map/bkgqs,bskd->bkgqd/dot_general | solution.py:44
  252.9 12.8 %divide_convert_fusion = bf16[16,512,128]{1,2,0:T(8,128)(2,1)S(1)} fusion(f32[16,512,128]{1,2,0:T(8,128)} %fusion.15, f32[16,512,128]{1,2,0:T(8,128)} %fusion.17, f32[16,512,128]{1,2,0:T(8,128)} %fusion.19, f32[16,512]{1,0:T(8,128)S(1)} %get-tuple-element.109, f32[16,512]{1,0:T(8,128)S(1)} %copy-done.26, f32[16,512]{1,0:T(8,128)S(1)} %copy-done.25, ...), kind=kOutput, calls=%fused_computation.113 | convolution fusion | flops 1099956224 | bytes 34013184 | tf_op jit(solution)/shard_map/bkgqs,bskd->bkgqd/dot_general | solution.py:44
  283.3 10.4 fusion.320
  293.8 12.0 %multiply_convert_fusion.4 = bf16[4,384,1024]{2,1,0:T(8,128)(2,1)} fusion(f32[4,384,1024]{2,1,0:T(8,128)S(1)} %fusion.320, bf16[4,384,2048]{2,1,0:T(8,128)(2,1)S(1)} %bitcast.380, bf16[4,2048,1024]{2,1,0:T(8,128)(2,1)} %param.31), kind=kOutput, calls=%fused_computation.70 | convolution fusion | flops 6451888128 | bytes 32505856 | tf_op jit(solution)/shard_map/ecd,edf->ecf/dot_general | solution.py:102
  305.8 15.3 %convolution_convert_fusion.3 = bf16[4,384,2048]{2,1,0:T(8,128)(2,1)} fusion(bf16[4,384,1024]{2,1,0:T(8,128)(2,1)} %multiply_convert_fusion.4, bf16[4,1024,2048]{2,1,0:T(8,128)(2,1)} %param.32), kind=kOutput, calls=%fused_computation.83 | convolution fusion | flops 6445596672 | bytes 26214400 | tf_op jit(solution)/shard_map/ecf,efd->ecd/dot_general | solution.py:104
  329.1 12.0 %fusion.321 = f32[4,384,1024]{2,1,0:T(8,128)} fusion(bf16[4,384,2048]{2,1,0:T(8,128)(2,1)S(1)} %bitcast.382, bf16[4,2048,1024]{2,1,0:T(8,128)(2,1)} %param.30), kind=kOutput, calls=%fused_computation.489 | convolution fusion | flops 6442450944 | bytes 29360128 | tf_op jit(solution)/shard_map/ecd,edf->ecf/dot_general | solution.py:101
  341.1 15.8 %multiply_convert_fusion.3 = bf16[4,384,1024]{2,1,0:T(8,128)(2,1)} fusion(f32[4,384,1024]{2,1,0:T(8,128)} %fusion.321, bf16[4,384,2048]{2,1,0:T(8,128)(2,1)S(1)} %bitcast.383, bf16[4,2048,1024]{2,1,0:T(8,128)(2,1)} %param.31), kind=kOutput, calls=%fused_computation.69 | convolution fusion | flops 6451888128 | bytes 32505856 | tf_op jit(solution)/shard_map/ecd,edf->ecf/dot_general | solution.py:102
  359.6 166.3 %collective-permute-start.3 = (bf16[384,2048]{1,0:T(8,128)(2,1)}, bf16[384,2048]{1,0:T(8,128)(2,1)S(1)}, u32[]{:S(2)}, u32[]{:S(2)}) collective-permute-start(bf16[384,2048]{1,0:T(8,128)(2,1)} %bitcast.104), channel_id=1, source_target_pairs={{0,1},{1,0},{2,3},{3,2},{4,5},{5,4},{6,7},{7,6},{8,9},{9,8},{10,11... | collective-permute-start | bytes 4718600 | tf_op jit(solution)/shard_map/ppermute | solution.py:183
  529.0 13.2 %convolution_convert_fusion.2 = bf16[4,384,2048]{2,1,0:T(8,128)(2,1)S(1)} fusion(bf16[4,384,1024]{2,1,0:T(8,128)(2,1)S(1)} %copy-done.34, bf16[4,1024,2048]{2,1,0:T(8,128)(2,1)} %param.32), kind=kOutput, calls=%fused_computation.82 | convolution fusion | flops 6445596672 | bytes 26214400 | tf_op jit(solution)/shard_map/ecf,efd->ecd/dot_general | solution.py:104
  546.4 17.9 %collective-permute-done.4 = bf16[384,2048]{1,0:T(8,128)(2,1)S(1)} collective-permute-done((bf16[384,2048]{1,0:T(8,128)(2,1)}, bf16[384,2048]{1,0:T(8,128)(2,1)S(1)}, u32[]{:S(2)}, u32[]{:S(2)}) %collective-permute-start.4) | collective-permute-done | bytes 1572896 | tf_op jit(solution)/shard_map/ppermute | solution.py:183
  564.3 33.3 %collective-permute-done.5 = bf16[384,2048]{1,0:T(8,128)(2,1)S(1)} collective-permute-done((bf16[384,2048]{1,0:T(8,128)(2,1)S(1)}, bf16[384,2048]{1,0:T(8,128)(2,1)S(1)}, u32[]{:S(2)}, u32[]{:S(2)}) %collective-permute-start.5) | collective-permute-done | bytes 1572896 | tf_op jit(solution)/shard_map/ppermute | solution.py:183
  598.7 12.2 %fusion.322 = f32[1536,2048]{1,0:T(8,128)} fusion(bf16[1536,1536]{1,0:T(8,128)(2,1)S(1)} %bitcast.422, bf16[1536,2048]{1,0:T(8,128)(2,1)S(1)} %pad_maximum_fusion), kind=kOutput, calls=%fused_computation.490 | convolution fusion | flops 9663676416 | bytes 23592960 | tf_op jit(solution)/shard_map/dot_general | solution.py:189
  633.4 15.6 %fusion.323 = f32[4,384,1024]{2,1,0:T(8,128)} fusion(bf16[4,384,2048]{2,1,0:T(8,128)(2,1)} %bitcast.385, bf16[4,2048,1024]{2,1,0:T(8,128)(2,1)} %param.30), kind=kOutput, calls=%fused_computation.491 | convolution fusion | flops 6442450944 | bytes 29360128 | tf_op jit(solution)/shard_map/ecd,edf->ecf/dot_general | solution.py:101
  649.0 15.7 %multiply_convert_fusion.2 = bf16[4,384,1024]{2,1,0:T(8,128)(2,1)} fusion(f32[4,384,1024]{2,1,0:T(8,128)} %fusion.323, bf16[4,384,2048]{2,1,0:T(8,128)(2,1)S(1)} %bitcast.386, bf16[4,2048,1024]{2,1,0:T(8,128)(2,1)} %param.31), kind=kOutput, calls=%fused_computation.68 | convolution fusion | flops 6451888128 | bytes 32505856 | tf_op jit(solution)/shard_map/ecd,edf->ecf/dot_general | solution.py:102
  664.7 14.8 %convolution_convert_fusion.1 = bf16[4,384,2048]{2,1,0:T(8,128)(2,1)} fusion(bf16[4,384,1024]{2,1,0:T(8,128)(2,1)} %multiply_convert_fusion.2, bf16[4,1024,2048]{2,1,0:T(8,128)(2,1)} %param.32), kind=kOutput, calls=%fused_computation.81 | convolution fusion | flops 6445596672 | bytes 26214400 | tf_op jit(solution)/shard_map/ecf,efd->ecd/dot_general | solution.py:104
  679.5 9.7 pad_maximum_fusion.1
  689.3 13.0 %fusion.324 = f32[1536,2048]{1,0:T(8,128)} fusion(bf16[1536,1536]{1,0:T(8,128)(2,1)S(1)} %bitcast.419, bf16[1536,2048]{1,0:T(8,128)(2,1)S(1)} %pad_maximum_fusion.1), kind=kOutput, calls=%fused_computation.492 | convolution fusion | flops 9663676416 | bytes 23592960 | tf_op jit(solution)/shard_map/dot_general | solution.py:189
  724.4 15.2 %fusion.325 = f32[4,384,1024]{2,1,0:T(8,128)} fusion(bf16[4,384,2048]{2,1,0:T(8,128)(2,1)} %bitcast.387, bf16[4,2048,1024]{2,1,0:T(8,128)(2,1)} %param.30), kind=kOutput, calls=%fused_computation.493 | convolution fusion | flops 6442450944 | bytes 29360128 | tf_op jit(solution)/shard_map/ecd,edf->ecf/dot_general | solution.py:101
  739.6 16.6 %multiply_convert_fusion.1 = bf16[4,384,1024]{2,1,0:T(8,128)(2,1)} fusion(f32[4,384,1024]{2,1,0:T(8,128)} %fusion.325, bf16[4,384,2048]{2,1,0:T(8,128)(2,1)} %bitcast.388, bf16[4,2048,1024]{2,1,0:T(8,128)(2,1)} %param.31), kind=kOutput, calls=%fused_computation.67 | convolution fusion | flops 6451888128 | bytes 32505856 | tf_op jit(solution)/shard_map/ecd,edf->ecf/dot_general | solution.py:102
  763.8 14.3 %convolution_convert_fusion = bf16[4,384,2048]{2,1,0:T(8,128)(2,1)} fusion(bf16[4,384,1024]{2,1,0:T(8,128)(2,1)S(1)} %copy-done.35, bf16[4,1024,2048]{2,1,0:T(8,128)(2,1)} %param.32), kind=kOutput, calls=%fused_computation.80 | convolution fusion | flops 6445596672 | bytes 26214400 | tf_op jit(solution)/shard_map/ecf,efd->ecd/dot_general | solution.py:104
  799.3 33.4 %collective-permute-done.13 = bf16[384,2048]{1,0:T(8,128)(2,1)} collective-permute-done((bf16[384,2048]{1,0:T(8,128)(2,1)}, bf16[384,2048]{1,0:T(8,128)(2,1)}, u32[]{:S(2)}, u32[]{:S(2)}) %collective-permute-start.13) | collective-permute-done | bytes 1572896 | tf_op jit(solution)/shard_map/ppermute | solution.py:183
  835.3 11.9 %fusion.326 = f32[1536,2048]{1,0:T(8,128)S(1)} fusion(bf16[1536,1536]{1,0:T(8,128)(2,1)} %bitcast.416, bf16[1536,2048]{1,0:T(8,128)(2,1)S(1)} %pad_maximum_fusion.2), kind=kOutput, calls=%fused_computation.494 | convolution fusion | flops 9663676416 | bytes 23592960 | tf_op jit(solution)/shard_map/dot_general | solution.py:189
  857.0 27.1 %fusion.113 = f32[512,8192]{1,0:T(8,128)} fusion(bf16[2048,8192]{1,0:T(8,128)(2,1)} %param.25, bf16[1,512,2048]{2,1,0:T(8,128)(2,1)S(1)} %copy-done.13, f32[2048]{0:T(1024)S(1)} %copy-done.30, f32[512]{0:T(512)S(1)} %add_rsqrt_fusion), kind=kOutput, calls=%fused_computation.168 | convolution fusion | flops 17184063488 | bytes 52439040 | tf_op jit(solution)/shard_map/dot_general | solution.py:218
  884.1 31.5 %fusion.12 = bf16[1,512,8192]{2,1,0:T(8,128)(2,1)} fusion(bf16[2048,8192]{1,0:T(8,128)(2,1)} %param.26, f32[512,8192]{1,0:T(8,128)} %fusion.113, bf16[1,512,2048]{2,1,0:T(8,128)(2,1)S(1)} %copy-done.13, f32[2048]{0:T(1024)S(1)} %copy-done.30, f32[512]{0:T(512)S(1)} %add_rsqrt_fusion), kind=kOutput, calls=%fused_computation.21 | convolution fusion | flops 17209229312 | bytes 60827648 | tf_op jit(solution)/shard_map/dot_general | solution.py:218
  915.6 29.7 %collective-permute-done.15 = f32[512,2048]{1,0:T(8,128)} collective-permute-done((f32[512,2048]{1,0:T(8,128)}, f32[512,2048]{1,0:T(8,128)}, u32[]{:S(2)}, u32[]{:S(2)}) %collective-permute-start.15) | collective-permute-done | bytes 4194336 | tf_op jit(solution)/shard_map/ppermute | solution.py:198
  945.3 11.9 %select_add_fusion = (f32[512,2048]{1,0:T(8,128)}, f32[512,2048]{1,0:T(8,128)}) fusion(f32[512,2048]{1,0:T(8,128)} %collective-permute-done.15, f32[512,2048]{1,0:T(8,128)} %copy-done.12, f32[512,2048]{1,0:T(8,128)} %slice_add_fusion.2, pred[]{:T(512)S(6)} %eq.567, f32[512,2048]{1,0:T(8,128)} %collective-permute-done.14, pred[]{:T(512)S(6)} %eq.566), kind=kLoop, calls=%fused_computation.111 | loop fusion | flops 4194304 | bytes 25165826 | tf_op jit(solution)/shard_map/add | solution.py:220
  960.6 12.3 %fusion.327 = f32[1536,2048]{1,0:T(8,128)S(1)} fusion(bf16[1536,1536]{1,0:T(8,128)(2,1)} %bitcast.415, bf16[1536,2048]{1,0:T(8,128)(2,1)S(1)} %pad_maximum_fusion.3), kind=kOutput, calls=%fused_computation.495 | convolution fusion | flops 9663676416 | bytes 23592960 | tf_op jit(solution)/shard_map/dot_general | solution.py:189
  981.4 24.6 %fusion.83 = bf16[1,512,2048]{2,1,0:T(8,128)(2,1)} fusion(bf16[8192,2048]{1,0:T(8,128)(2,1)} %param.27, bf16[1,512,8192]{2,1,0:T(8,128)(2,1)} %fusion.12), kind=kOutput, calls=%fused_computation.132 | convolution fusion | flops 17180917760 | bytes 44040192 | tf_op jit(solution)/shard_map/dot_general | solution.py:34
  1006.0 62.2 %collective-permute-done.19 = f32[512,2048]{1,0:T(8,128)} collective-permute-done((f32[512,2048]{1,0:T(8,128)}, f32[512,2048]{1,0:T(8,128)}, u32[]{:S(2)}, u32[]{:S(2)}) %collective-permute-start.19) | collective-permute-done | bytes 4194336 | tf_op jit(solution)/shard_map/ppermute | solution.py:195
  (257 shorter events, 324.0 us)
Async XLA Ops:
  6.5 268.3 %all-gather.4.cloned.1.call-start = ((), (), s32[]{:S(2)}) async-start(), calls=%async_computation | async-start | bytes 35651584 | tf_op jit(solution)/shard_map/all_gather | solution.py:137
  10.2 26.0 %copy-start.4 = (bf16[1,512,2048]{2,1,0:T(8,128)(2,1)S(1)}, bf16[1,512,2048]{2,1,0:T(8,128)(2,1)}, u32[]{:S(2)}) copy-start(bf16[1,512,2048]{2,1,0:T(8,128)(2,1)} %param.17) | copy-start | bytes 6291460
  83.5 16.7 %collective-permute-start = (bf16[2,1,512,16,128]{4,2,3,1,0:T(8,128)(2,1)}, bf16[2,1,512,16,128]{4,2,3,1,0:T(8,128)(2,1)}, u32[]{:S(2)}, u32[]{:S(2)}) collective-permute-start(bf16[2,1,512,16,128]{4,2,3,1,0:T(8,128)(2,1)} %pad_maximum_fusion.4), channel_id=1, source_target_pairs={{0,1},{1,2},{2,3},{4,5},{5,6},{6,7},{8,9},{9,10},{10,11},{12,13},{... | collective-permute-start | bytes 12582920 | tf_op jit(solution)/shard_map/ppermute | solution.py:147
  100.2 24.5 %collective-permute-start.1 = (bf16[2,1,512,16,128]{4,2,3,1,0:T(8,128)(2,1)}, bf16[2,1,512,16,128]{4,2,3,1,0:T(8,128)(2,1)}, u32[]{:S(2)}, u32[]{:S(2)}) collective-permute-start(bf16[2,1,512,16,128]{4,2,3,1,0:T(8,128)(2,1)} %collective-permute-done), channel_id=1, source_target_pairs={{1,2},{2,3},{5,6},{6,7},{9,10},{10,11},{13,14},{14,15},{17,18},{18... | collective-permute-start | bytes 12582920 | tf_op jit(solution)/shard_map/ppermute | solution.py:147
  124.7 42.9 %collective-permute-start.2 = (bf16[2,1,512,16,128]{4,2,3,1,0:T(8,128)(2,1)}, bf16[2,1,512,16,128]{4,2,3,1,0:T(8,128)(2,1)}, u32[]{:S(2)}, u32[]{:S(2)}) collective-permute-start(bf16[2,1,512,16,128]{4,2,3,1,0:T(8,128)(2,1)} %collective-permute-done.1), channel_id=1, source_target_pairs={{2,3},{6,7},{10,11},{14,15},{18,19},{22,23},{26,27},{30,31}} | collective-permute-start | bytes 12582920 | tf_op jit(solution)/shard_map/ppermute | solution.py:147
  329.1 27.9 %slice-start = ((s8[6291456]{0:T(1024)(128)(4,1)}), s8[4194304]{0:T(1024)(128)(4,1)S(1)}, s32[]{:S(2)}) async-start(s8[6291456]{0:T(1024)(128)(4,1)} %bitcast.390), calls=%async_computation.1 | async-start | bytes 8388608
  357.0 172.0 %copy-start.34 = (bf16[4,384,1024]{2,1,0:T(8,128)(2,1)S(1)}, bf16[4,384,1024]{2,1,0:T(8,128)(2,1)}, u32[]{:S(2)}) copy-start(bf16[4,384,1024]{2,1,0:T(8,128)(2,1)} %multiply_convert_fusion.3) | copy-start | bytes 9437188
  359.6 186.8 %collective-permute-start.3 = (bf16[384,2048]{1,0:T(8,128)(2,1)}, bf16[384,2048]{1,0:T(8,128)(2,1)S(1)}, u32[]{:S(2)}, u32[]{:S(2)}) collective-permute-start(bf16[384,2048]{1,0:T(8,128)(2,1)} %bitcast.104), channel_id=1, source_target_pairs={{0,1},{1,0},{2,3},{3,2},{4,5},{5,4},{6,7},{7,6},{8,9},{9,8},{10,11... | collective-permute-start | bytes 4718600 | tf_op jit(solution)/shard_map/ppermute | solution.py:183
  525.9 38.4 %collective-permute-start.4 = (bf16[384,2048]{1,0:T(8,128)(2,1)}, bf16[384,2048]{1,0:T(8,128)(2,1)S(1)}, u32[]{:S(2)}, u32[]{:S(2)}) collective-permute-start(bf16[384,2048]{1,0:T(8,128)(2,1)} %bitcast.105), channel_id=1, source_target_pairs={{0,2},{1,3},{2,0},{3,1},{4,6},{5,7},{6,4},{7,5},{8,10},{9,11},{10,... | collective-permute-start | bytes 4718600 | tf_op jit(solution)/shard_map/ppermute | solution.py:183
  528.8 68.8 %collective-permute-start.5 = (bf16[384,2048]{1,0:T(8,128)(2,1)S(1)}, bf16[384,2048]{1,0:T(8,128)(2,1)S(1)}, u32[]{:S(2)}, u32[]{:S(2)}) collective-permute-start(bf16[384,2048]{1,0:T(8,128)(2,1)S(1)} %bitcast.401), channel_id=1, source_target_pairs={{0,3},{1,2},{2,1},{3,0},{4,7},{5,6},{6,5},{7,4},{8,11},{9,10},{10,... | collective-permute-start | bytes 4718600 | tf_op jit(solution)/shard_map/ppermute | solution.py:183
  544.3 135.2 %collective-permute-start.6 = (bf16[384,2048]{1,0:T(8,128)(2,1)}, bf16[384,2048]{1,0:T(8,128)(2,1)S(1)}, u32[]{:S(2)}, u32[]{:S(2)}) collective-permute-start(bf16[384,2048]{1,0:T(8,128)(2,1)} %bitcast.113), channel_id=1, source_target_pairs={{0,1},{1,0},{2,3},{3,2},{4,5},{5,4},{6,7},{7,6},{8,9},{9,8},{10,11... | collective-permute-start | bytes 4718600 | tf_op jit(solution)/shard_map/ppermute | solution.py:183
  544.4 135.0 %collective-permute-start.7 = (bf16[384,2048]{1,0:T(8,128)(2,1)}, bf16[384,2048]{1,0:T(8,128)(2,1)}, u32[]{:S(2)}, u32[]{:S(2)}) collective-permute-start(bf16[384,2048]{1,0:T(8,128)(2,1)} %bitcast.114), channel_id=1, source_target_pairs={{0,2},{1,3},{2,0},{3,1},{4,6},{5,7},{6,4},{7,5},{8,10},{9,11},{10,... | collective-permute-start | bytes 4718600 | tf_op jit(solution)/shard_map/ppermute | solution.py:183
  546.4 52.3 %slice-start.8 = ((s8[4718592]{0:T(1024)(128)(4,1)}), s8[4194304]{0:T(1024)(128)(4,1)S(1)}, s32[]{:S(2)}) async-start(s8[4718592]{0:T(1024)(128)(4,1)} %bitcast.420), calls=%async_computation.9 | async-start | bytes 8388608
  546.4 52.3 %slice-start.9 = ((s8[4718592]{0:T(1024)(128)(4,1)}), s8[524288]{0:T(1024)(128)(4,1)S(1)}, s32[]{:S(2)}) async-start(s8[4718592]{0:T(1024)(128)(4,1)} %bitcast.420), calls=%async_computation.10 | async-start | bytes 1048576
  546.4 133.1 %collective-permute-start.8 = (bf16[384,2048]{1,0:T(8,128)(2,1)}, bf16[384,2048]{1,0:T(8,128)(2,1)}, u32[]{:S(2)}, u32[]{:S(2)}) collective-permute-start(bf16[384,2048]{1,0:T(8,128)(2,1)} %bitcast.115), channel_id=1, source_target_pairs={{0,3},{1,2},{2,1},{3,0},{4,7},{5,6},{6,5},{7,4},{8,11},{9,10},{10,... | collective-permute-start | bytes 4718600 | tf_op jit(solution)/shard_map/ppermute | solution.py:183
  616.9 167.2 %collective-permute-start.10 = (f32[512,2048]{1,0:T(8,128)S(1)}, f32[512,2048]{1,0:T(8,128)}, u32[]{:S(2)}, u32[]{:S(2)}) collective-permute-start(f32[512,2048]{1,0:T(8,128)S(1)} %slice_add_fusion.6), channel_id=1, source_target_pairs={{12,8},{13,9},{14,10},{15,11},{28,24},{29,25},{30,26},{31,27}} | collective-permute-start | bytes 12582920 | tf_op jit(solution)/shard_map/ppermute | solution.py:198
  620.2 164.0 %collective-permute-start.9 = (f32[512,2048]{1,0:T(8,128)S(1)}, f32[512,2048]{1,0:T(8,128)}, u32[]{:S(2)}, u32[]{:S(2)}) collective-permute-start(f32[512,2048]{1,0:T(8,128)S(1)} %slice_add_fusion.6), channel_id=1, source_target_pairs={{0,4},{1,5},{2,6},{3,7},{16,20},{17,21},{18,22},{19,23}} | collective-permute-start | bytes 12582920 | tf_op jit(solution)/shard_map/ppermute | solution.py:195
  761.6 33.0 %collective-permute-start.11 = (bf16[384,2048]{1,0:T(8,128)(2,1)}, bf16[384,2048]{1,0:T(8,128)(2,1)S(1)}, u32[]{:S(2)}, u32[]{:S(2)}) collective-permute-start(bf16[384,2048]{1,0:T(8,128)(2,1)} %bitcast.122), channel_id=1, source_target_pairs={{0,1},{1,0},{2,3},{3,2},{4,5},{5,4},{6,7},{7,6},{8,9},{9,8},{10,11... | collective-permute-start | bytes 4718600 | tf_op jit(solution)/shard_map/ppermute | solution.py:183
  761.8 37.5 %collective-permute-start.12 = (bf16[384,2048]{1,0:T(8,128)(2,1)}, bf16[384,2048]{1,0:T(8,128)(2,1)S(1)}, u32[]{:S(2)}, u32[]{:S(2)}) collective-permute-start(bf16[384,2048]{1,0:T(8,128)(2,1)} %bitcast.123), channel_id=1, source_target_pairs={{0,2},{1,3},{2,0},{3,1},{4,6},{5,7},{6,4},{7,5},{8,10},{9,11},{10,... | collective-permute-start | bytes 4718600 | tf_op jit(solution)/shard_map/ppermute | solution.py:183
  763.8 68.8 %collective-permute-start.13 = (bf16[384,2048]{1,0:T(8,128)(2,1)}, bf16[384,2048]{1,0:T(8,128)(2,1)}, u32[]{:S(2)}, u32[]{:S(2)}) collective-permute-start(bf16[384,2048]{1,0:T(8,128)(2,1)} %bitcast.124), channel_id=1, source_target_pairs={{0,3},{1,2},{2,1},{3,0},{4,7},{5,6},{6,5},{7,4},{8,11},{9,10},{10,... | collective-permute-start | bytes 4718600 | tf_op jit(solution)/shard_map/ppermute | solution.py:183
  784.1 173.2 %collective-permute-start.16 = (bf16[384,2048]{1,0:T(8,128)(2,1)}, bf16[384,2048]{1,0:T(8,128)(2,1)}, u32[]{:S(2)}, u32[]{:S(2)}) collective-permute-start(bf16[384,2048]{1,0:T(8,128)(2,1)} %bitcast.130), channel_id=1, source_target_pairs={{0,1},{1,0},{2,3},{3,2},{4,5},{5,4},{6,7},{7,6},{8,9},{9,8},{10,11... | collective-permute-start | bytes 4718600 | tf_op jit(solution)/shard_map/ppermute | solution.py:183
  784.2 173.1 %collective-permute-start.17 = (bf16[384,2048]{1,0:T(8,128)(2,1)}, bf16[384,2048]{1,0:T(8,128)(2,1)}, u32[]{:S(2)}, u32[]{:S(2)}) collective-permute-start(bf16[384,2048]{1,0:T(8,128)(2,1)} %bitcast.131), channel_id=1, source_target_pairs={{0,2},{1,3},{2,0},{3,1},{4,6},{5,7},{6,4},{7,5},{8,10},{9,11},{10,... | collective-permute-start | bytes 4718600 | tf_op jit(solution)/shard_map/ppermute | solution.py:183
  794.6 162.6 %collective-permute-start.18 = (bf16[384,2048]{1,0:T(8,128)(2,1)}, bf16[384,2048]{1,0:T(8,128)(2,1)}, u32[]{:S(2)}, u32[]{:S(2)}) collective-permute-start(bf16[384,2048]{1,0:T(8,128)(2,1)} %bitcast.132), channel_id=1, source_target_pairs={{0,3},{1,2},{2,1},{3,0},{4,7},{5,6},{6,5},{7,4},{8,11},{9,10},{10,... | collective-permute-start | bytes 4718600 | tf_op jit(solution)/shard_map/ppermute | solution.py:183
  850.5 65.1 %collective-permute-start.14 = (f32[512,2048]{1,0:T(8,128)}, f32[512,2048]{1,0:T(8,128)}, u32[]{:S(2)}, u32[]{:S(2)}) collective-permute-start(f32[512,2048]{1,0:T(8,128)} %get-tuple-element.87), channel_id=1, source_target_pairs={{0,4},{4,8},{1,5},{5,9},{2,6},{6,10},{3,7},{7,11},{16,20},{20,24},... | collective-permute-start | bytes 12582920 | tf_op jit(solution)/shard_map/ppermute | solution.py:195
  853.2 92.1 %collective-permute-start.15 = (f32[512,2048]{1,0:T(8,128)}, f32[512,2048]{1,0:T(8,128)}, u32[]{:S(2)}, u32[]{:S(2)}) collective-permute-start(f32[512,2048]{1,0:T(8,128)} %get-tuple-element.88), channel_id=1, source_target_pairs={{12,8},{8,4},{13,9},{9,5},{14,10},{10,6},{15,11},{11,7},{28,24},{2... | collective-permute-start | bytes 12582920 | tf_op jit(solution)/shard_map/ppermute | solution.py:198
  915.6 41.7 %copy-start.18 = (bf16[4,1,96,2048]{3,2,1,0:T(8,128)(2,1)S(1)}, bf16[4,1,96,2048]{3,2,1,0:T(8,128)(2,1)}, u32[]{:S(2)}) copy-start(bf16[4,1,96,2048]{3,2,1,0:T(8,128)(2,1)} %get-tuple-element.123) | copy-start | bytes 4718596
  972.9 96.2 %copy-start.5 = (bf16[1,512,2048]{2,1,0:T(8,128)(2,1)S(1)}, bf16[1,512,2048]{2,1,0:T(8,128)(2,1)}, u32[]{:S(2)}) copy-start(bf16[1,512,2048]{2,1,0:T(8,128)(2,1)} %param.17) | copy-start | bytes 6291460
  972.9 96.2 %copy-start.24 = (f32[2048]{0:T(1024)S(1)}, f32[2048]{0:T(1024)}, u32[]{:S(2)}) copy-start(f32[2048]{0:T(1024)} %copy-done.23) | copy-start | bytes 24580
  972.9 96.2 %copy-start.28 = (f32[512]{0:T(512)S(1)}, f32[512]{0:T(512)}, u32[]{:S(2)}) copy-start(f32[512]{0:T(512)} %copy-done.27) | copy-start | bytes 6148
  972.9 96.2 %copy-start.29 = (f32[512]{0:T(512)S(1)}, f32[512]{0:T(512)}, u32[]{:S(2)}) copy-start(f32[512]{0:T(512)} %get-tuple-element.107) | copy-start | bytes 6148
  973.0 95.3 %collective-permute-start.19 = (f32[512,2048]{1,0:T(8,128)}, f32[512,2048]{1,0:T(8,128)}, u32[]{:S(2)}, u32[]{:S(2)}) collective-permute-start(f32[512,2048]{1,0:T(8,128)} %get-tuple-element.93), channel_id=1, source_target_pairs={{0,4},{4,8},{8,12},{1,5},{5,9},{9,13},{2,6},{6,10},{10,14},{3,7},{... | collective-permute-start | bytes 12582920 | tf_op jit(solution)/shard_map/ppermute | solution.py:195
  974.4 94.7 %collective-permute-start.20 = (f32[512,2048]{1,0:T(8,128)S(1)}, f32[512,2048]{1,0:T(8,128)}, u32[]{:S(2)}, u32[]{:S(2)}) collective-permute-start(f32[512,2048]{1,0:T(8,128)S(1)} %copy-done.19), channel_id=1, source_target_pairs={{12,8},{8,4},{4,0},{13,9},{9,5},{5,1},{14,10},{10,6},{6,2},{15,11}... | collective-permute-start | bytes 12582920 | tf_op jit(solution)/shard_map/ppermute | solution.py:198
  (36 other events, 302.8 us)
Sparse Core Ops, SparseCore 0:
  36.3 220.7 all-gather.3
